TPU v7x, 8 devices: a whole 2x2x1 slice. The times are simulated.
8 devices in a mesh: dp: 2 (over z, y), ep: 4 (over x, core).
Axes of the slice: x: 2, y: 2, z: 1, core: 2. Of those that a mesh axis runs over, the one named last changes fastest.
Arguments:
- tokens: bfloat16 [2048, 2048], P(('dp', 'ep')), parts along dimension 0
- expert_ids: int32 [2048, 8], P(('dp', 'ep')), parts along dimension 0
- gate_vals: float32 [2048, 8], P(('dp', 'ep')), parts along dimension 0
- w_gate: bfloat16 [64, 2048, 1024], P('ep')
- w_up: bfloat16 [64, 2048, 1024], P('ep')
- w_down: bfloat16 [64, 1024, 2048], P('ep')
Outputs:
- output: bfloat16 [2048, 2048], P(('dp', 'ep')), parts along dimension 0
There are 2 independent parts. A program takes and returns all parts, laid end to end along the dimension named above; an argument that names none is the same for every part.
All inputs are finite; a program needn't handle non-finite values.
Results may differ from a plain program's by a relative error of at most 0.0063039.
Values are sent between devices in bfloat16 or wider.
A program may use at most 1 GiB of HBM per device.

v0:
```python
import jax
import jax.numpy as jnp
from jax import lax
from jax.sharding import PartitionSpec as P, NamedSharding


def expert_ffn(expert_in, w_gate, w_up, w_down):
    gate_act = jnp.einsum('lcd,ldf->lcf', expert_in, w_gate, preferred_element_type=jnp.float32)
    up_act = jnp.einsum('lcd,ldf->lcf', expert_in, w_up, preferred_element_type=jnp.float32)
    hidden = (jax.nn.silu(gate_act) * up_act).astype(jnp.bfloat16)
    return jnp.einsum('lcf,lfd->lcd', hidden, w_down, preferred_element_type=jnp.float32).astype(jnp.bfloat16)


def serve_rows(recv_rows, recv_gate, w_gate, w_up, w_down, expert_cap):
    member = recv_gate != 0.0
    exp_slot = jnp.cumsum(member.astype(jnp.int32), axis=0) - 1
    fan_mat = (member.T[:, None, :] & (exp_slot.T[:, None, :] == jnp.arange(expert_cap)[None, :, None])).astype(jnp.bfloat16)
    expert_in = jnp.einsum('lcr,rd->lcd', fan_mat, recv_rows, preferred_element_type=jnp.float32).astype(jnp.bfloat16)
    expert_out = expert_ffn(expert_in, w_gate, w_up, w_down)
    row_outs = jnp.einsum('lcr,lcd->lrd', fan_mat, expert_out, preferred_element_type=jnp.float32)
    dev_sum = jnp.sum(recv_gate.T[:, :, None] * row_outs, axis=0)
    return dev_sum.astype(jnp.bfloat16)


def send_tables(expert_ids, gate_vals, groups, local_count, pair_cap):
    tok_dev = expert_ids.shape[0]
    chosen = jnp.any((expert_ids // local_count)[:, :, None] == jnp.arange(groups)[None, None, :], axis=1)
    send_rank = jnp.cumsum(chosen.astype(jnp.int32), axis=0) - 1
    pack_mask = chosen.T[:, None, :] & (send_rank.T[:, None, :] == jnp.arange(pair_cap)[None, :, None])
    gate_dense = jnp.sum(jnp.where(expert_ids[:, :, None] == jnp.arange(groups * local_count)[None, None, :], gate_vals[:, :, None], 0.0), axis=1)
    gate_t = jnp.swapaxes(gate_dense.reshape(tok_dev, groups, local_count), 0, 1)
    send_gate = jnp.sum(jnp.where(pack_mask[:, :, :, None], gate_t[:, None, :, :], 0.0), axis=2)
    return pack_mask.astype(jnp.bfloat16), send_gate


def solution(mesh):
    groups = mesh.shape['ep']
    row_spec = P(('dp', 'ep'))
    expert_spec = P('ep')

    def device_step(tokens, expert_ids, gate_vals, w_gate, w_up, w_down):
        tok_dev, top_k = expert_ids.shape
        d_model = tokens.shape[1]
        local_count = w_gate.shape[0]
        pair_cap = tok_dev * (top_k // 2) // groups
        expert_cap = tok_dev * top_k // local_count
        row_count = groups * pair_cap
        pack_mat, send_gate = send_tables(expert_ids, gate_vals, groups, local_count, pair_cap)
        send_rows = jnp.einsum('qct,td->qcd', pack_mat, tokens, preferred_element_type=jnp.float32).astype(jnp.bfloat16)
        recv_rows = lax.all_to_all(send_rows, 'ep', 0, 0, tiled=True)
        recv_gate = lax.all_to_all(send_gate, 'ep', 0, 0, tiled=True)
        dev_sum = serve_rows(recv_rows.reshape(row_count, d_model), recv_gate.reshape(row_count, local_count), w_gate, w_up, w_down, expert_cap)
        returned = lax.all_to_all(dev_sum.reshape(groups, pair_cap, d_model), 'ep', 0, 0, tiled=True)
        moe_sum = jnp.einsum('qct,qcd->td', pack_mat, returned, preferred_element_type=jnp.float32)
        return (tokens.astype(jnp.float32) + moe_sum).astype(jnp.bfloat16)

    return jax.shard_map(device_step, mesh=mesh, in_specs=(row_spec, row_spec, row_spec, expert_spec, expert_spec, expert_spec), out_specs=row_spec, check_vma=False)
```

profile of v0, /device:TPU:0, one launch (start us, length us, event | category | flops | bytes accessed | tf_op | source)
XLA Modules:
  0.0 250.9 jit_solution(8288713991843653332)
XLA Ops:
  0.0 0.7 add_select_fusion
  0.8 1.2 reduce-window.14
  2.0 0.1 slice.16
  2.1 0.1 copy.51
  2.2 0.1 copy.52
  2.3 0.1 add_bitcast_fusion
  2.4 0.8 select_reduce_fusion.1
  3.2 0.3 fusion.19
  3.5 0.4 copy.53
  4.0 2.2 select_reduce_fusion
  6.2 0.8 copy.54
  7.0 4.6 %all-to-all-start = ((f32[4,256,16]{1,2,0:T(8,128)}), f32[4,256,16]{1,2,0:T(8,128)S(1)}, u32[]{:S(2)}, u32[]{:S(2)}) async-start(f32[4,256,16]{1,2,0:T(8,128)} %copy.54), calls=%async_computation | async-start | bytes 131072 | tf_op jit(solution)/shard_map/all_to_all | solution.py:51
  11.6 4.4 %convolution_convert_fusion = bf16[4,256,2048]{2,1,0:T(8,128)(2,1)} fusion(bf16[256,2048]{1,0:T(8,128)(2,1)} %param.6, s32[4,256]{1,0:T(4,128)S(1)} %bitcast.59, pred[4,256]{1,0:T(4,128)(4,1)S(1)} %bitcast.64), kind=kOutput, calls=%fused_computation.14 | convolution fusion | flops 1076363264 | bytes 5248000 | tf_op jit(solution)/shard_map/qct,td->qcd/dot_general | solution.py:49
  16.0 0.0 all-to-all-done
  16.0 5.1 %all-to-all-start.1 = ((bf16[4,256,2048]{2,1,0:T(8,128)(2,1)}), bf16[4,256,2048]{2,1,0:T(8,128)(2,1)}, u32[]{:S(2)}, u32[]{:S(2)}) async-start(bf16[4,256,2048]{2,1,0:T(8,128)(2,1)} %convolution_convert_fusion), calls=%async_computation.1 | async-start | bytes 8388608 | tf_op jit(solution)/shard_map/all_to_all | solution.py:50
  21.2 4.5 %reduce-window.16 = s32[16,8,128]{2,1,0:T(8,128)S(1)} reduce-window(s32[16,8,128]{2,1,0:T(8,128)S(1)} %bitcast.56, s32[]{:T(128)} %constant.27.clone.1), window={size=1x1x128 pad=0_0x0_0x127_0}, to_apply=%region_5.6 | reduce-window | flops 2080768 | bytes 131076 | tf_op jit(solution)/shard_map/reduce-window.2
  25.7 0.1 slice.17
  25.8 0.1 copy.56
  25.9 0.1 copy.57
  26.0 0.1 add_add_fusion
  26.1 42.8 %all-to-all-done.1 = bf16[4,256,2048]{2,1,0:T(8,128)(2,1)} async-done(((bf16[4,256,2048]{2,1,0:T(8,128)(2,1)}), bf16[4,256,2048]{2,1,0:T(8,128)(2,1)}, u32[]{:S(2)}, u32[]{:S(2)}) %all-to-all-start.1) | async-done | bytes 4194336 | tf_op jit(solution)/shard_map/all_to_all | solution.py:50
  68.9 14.4 %fusion.7 = bf16[16,128,2048]{2,1,0:T(8,128)(2,1)} fusion(bf16[1024,2048,1]{1,0,2:T(8,128)(2,1)} %bitcast.9, s32[16,1024]{1,0:T(8,128)S(1)} %bitcast.61, pred[16,1024]{1,0:T(8,128)(4,1)S(1)} %get-tuple-element.6), kind=kOutput, calls=%fused_computation.8 | convolution fusion | flops 8598323200 | bytes 12664832 | tf_op jit(solution)/shard_map/lcr,rd->lcd/dot_general | solution.py:18
  83.3 28.8 %fusion.28 = f32[16,128,1024]{2,1,0:T(8,128)} fusion(bf16[16,128,2048]{2,1,0:T(8,128)(2,1)} %fusion.7, bf16[16,2048,1024]{2,1,0:T(8,128)(2,1)} %param.10), kind=kOutput, calls=%fused_computation.41 | convolution fusion | flops 8589934592 | bytes 83886080 | tf_op jit(solution)/shard_map/lcd,ldf->lcf/dot_general | solution.py:9
  112.1 28.8 %fusion.27 = f32[16,128,1024]{2,1,0:T(8,128)} fusion(bf16[16,128,2048]{2,1,0:T(8,128)(2,1)} %fusion.7, bf16[16,2048,1024]{2,1,0:T(8,128)(2,1)} %param.9), kind=kOutput, calls=%fused_computation.40 | convolution fusion | flops 8589934592 | bytes 83886080 | tf_op jit(solution)/shard_map/lcd,ldf->lcf/dot_general | solution.py:8
  140.9 31.7 %fusion.46 = bf16[16,128,2048]{2,1,0:T(8,128)(2,1)} fusion(bf16[16,1024,2048]{2,1,0:T(8,128)(2,1)} %param.11, f32[16,128,1024]{2,1,0:T(8,128)} %fusion.28, f32[16,128,1024]{2,1,0:T(8,128)} %fusion.27), kind=kOutput, calls=%fused_computation.2.clone.2 | convolution fusion | flops 8606711808 | bytes 92274688 | tf_op jit(solution)/shard_map/lcf,lfd->lcd/dot_general | solution.py:11
  172.6 25.0 %multiply_reduce_fusion = bf16[1024,2048]{1,0:T(8,128)(2,1)S(1)} fusion(f32[16,1024]{1,0:T(8,128)S(1)} %bitcast.53, s32[16,1024]{1,0:T(8,128)S(1)} %bitcast.62, pred[16,1024]{1,0:T(8,128)(4,1)S(1)} %get-tuple-element.6, bf16[16,128,2048]{2,1,0:T(8,128)(2,1)} %fusion.46), kind=kOutput, calls=%fused_computation | convolution fusion | flops 8659140608 | bytes 12730368 | tf_op jit(solution)/shard_map/lcr,lcd->lrd/dot_general | solution.py:20
  197.6 0.0 copy-start
  197.6 50.8 %all_to_all.15 = bf16[4,256,2048]{2,1,0:T(8,128)(2,1)S(1)} all-to-all(bf16[4,256,2048]{2,1,0:T(8,128)(2,1)S(1)} %bitcast.51), channel_id=1, replica_groups=mesh['dp'=2,'ep'=4] {'ep'}, dimensions={0} | all-to-all | bytes 8388608 | tf_op jit(solution)/shard_map/all_to_all | solution.py:53
  248.4 0.0 copy-done
  248.4 2.5 fusion.17
  (12 shorter events, 0.2 us)
Async XLA Ops:
  7.0 9.0 %all-to-all-start = ((f32[4,256,16]{1,2,0:T(8,128)}), f32[4,256,16]{1,2,0:T(8,128)S(1)}, u32[]{:S(2)}, u32[]{:S(2)}) async-start(f32[4,256,16]{1,2,0:T(8,128)} %copy.54), calls=%async_computation | async-start | bytes 131072 | tf_op jit(solution)/shard_map/all_to_all | solution.py:51
  16.0 52.9 %all-to-all-start.1 = ((bf16[4,256,2048]{2,1,0:T(8,128)(2,1)}), bf16[4,256,2048]{2,1,0:T(8,128)(2,1)}, u32[]{:S(2)}, u32[]{:S(2)}) async-start(bf16[4,256,2048]{2,1,0:T(8,128)(2,1)} %convolution_convert_fusion), calls=%async_computation.1 | async-start | bytes 8388608 | tf_op jit(solution)/shard_map/all_to_all | solution.py:50
  197.6 50.8 %copy-start = (bf16[256,2048]{1,0:T(8,128)(2,1)S(1)}, bf16[256,2048]{1,0:T(8,128)(2,1)}, u32[]{:S(2)}) copy-start(bf16[256,2048]{1,0:T(8,128)(2,1)} %param.6) | copy-start | bytes 3145732
where the time goes:
time: 251 us
  matrix products  136 us (54%)
  blocking collectives  50.8 us (20%)
  waiting for transfers between devices  42.8 us (17%)
  other arithmetic  10.1 us (4%)
  starting transfers between devices  9.73 us (4%)
    all_to_all x1, blocking collectives, device_step(): lax.all_to_all(dev_sum.reshape(groups, pair_cap, d_model), 'ep', 0, 0, ti...  50.8 us
    all_to_all x1, waiting for transfers between devices, device_step(): recv_rows = lax.all_to_all(send_rows, 'ep', 0, 0, tiled=True)  42.8 us
    dot_general x1, matrix products, expert_ffn(): jnp.einsum('lcf,lfd->lcd', hidden, w_down, preferred_element_type=jnp.flo...  31.7 us
    dot_general x1, matrix products, expert_ffn(): jnp.einsum('lcd,ldf->lcf', expert_in, w_up, preferred_element_type=jnp.fl...  28.8 us
    dot_general x1, matrix products, expert_ffn(): jnp.einsum('lcd,ldf->lcf', expert_in, w_gate, preferred_element_type=jnp....  28.8 us
    dot_general x1, matrix products, serve_rows(): jnp.einsum('lcr,lcd->lrd', fan_mat, expert_out, preferred_element_type=jn...  25 us
    dot_general x1, matrix products, serve_rows(): jnp.einsum('lcr,rd->lcd', fan_mat, recv_rows, preferred_element_type=jnp....  14.4 us
    another operation x5, other arithmetic  5.81 us
  transfers between devices with their start and end apart: 2, of which 1 were waited for; matrix products, arithmetic and copies ran while one was open for 4% of the time, Pallas kernels for 0%

commit v1 on v0

v1 whole, which is shorter than its diff:
```python
import functools

import jax
import jax.numpy as jnp
from jax import lax
from jax.experimental import pallas as pl
from jax.experimental.pallas import tpu as pltpu
from jax.sharding import PartitionSpec as P

MESH = pl.DeviceIdType.MESH
F32, BF16 = jnp.float32, jnp.bfloat16
GROUPS = 4
CAP = 128
KB = 512
DB = 256
RING1 = 8
EPS = 4
RING2 = 4


def layer_kernel(tok, ids_in, gts_in, w_gate, w_up, w_down, out, acc, rows_all, own, hid, ring1, ring2, back, pick1, pick2,
                 y_blk, xbuf, ids_all, gts_all, slots, tbl, w1_sem, w2_sem, loc_sem, idx_send, idx_recv, d_send, d_recv,
                 r_send, r_recv, o_sem):
    tok_dev, d_model = tok.shape
    n_exp, _, ffn = w_gate.shape
    n_tok = GROUPS * tok_dev
    n_kb, n_db, n_grp = d_model // KB, d_model // DB, n_exp // EPS
    steps1, steps2 = n_kb * n_exp, n_db * n_grp

    me = lax.axis_index('ep')
    sib = me + 1 - 2 * lax.rem(me, 2)
    over = lax.rem(me + 2, GROUPS)
    diag = lax.rem(sib + 2, GROUPS)
    peers = (over, diag, sib)

    def rows_of(dev):
        return pl.ds(pl.multiple_of(dev * tok_dev, tok_dev), tok_dev)

    def w1_copies(step, slot):
        e, k = lax.rem(step, n_exp), lax.div(step, n_exp)
        rows = pl.ds(pl.multiple_of(k * KB, KB), KB)
        return (pltpu.make_async_copy(w_gate.at[e, rows, :], ring1.at[slot, 0], w1_sem.at[slot, 0]),
                pltpu.make_async_copy(w_up.at[e, rows, :], ring1.at[slot, 1], w1_sem.at[slot, 1]))

    def w2_copy(step, slot):
        g, d = lax.rem(step, n_grp), lax.div(step, n_grp)
        cols = pl.ds(pl.multiple_of(d * DB, DB), DB)
        return pltpu.make_async_copy(w_down.at[pl.ds(g * EPS, EPS), :, cols], ring2.at[slot], w2_sem.at[slot])

    own_copy = pltpu.make_async_copy(tok, own, loc_sem.at[0])
    mine_copy = pltpu.make_async_copy(tok, rows_all.at[rows_of(me), :], loc_sem.at[1])
    own_copy.start()
    mine_copy.start()

    def prefetch1(step, c):
        for copy in w1_copies(step, step):
            copy.start()
        return c

    lax.fori_loop(0, RING1, prefetch1, 0)

    def prefetch2(step, c):
        w2_copy(step, step).start()
        return c

    lax.fori_loop(0, RING2, prefetch2, 0)

    barrier = pltpu.get_barrier_semaphore()
    for dev in peers:
        pl.semaphore_signal(barrier, inc=1, device_id={'ep': dev}, device_id_type=MESH)
    pl.semaphore_wait(barrier, len(peers))

    def idx_copy(j, what):
        src, dst = (ids_in, ids_all) if what == 0 else (gts_in, gts_all)
        return pltpu.make_async_remote_copy(src_ref=src, dst_ref=dst.at[j], send_sem=idx_send.at[what, j], recv_sem=idx_recv.at[what, j],
                                            device_id={'ep': peers[j]}, device_id_type=MESH)

    def disp_copy(kind, k):
        cols = pl.ds(k * KB, KB) if isinstance(k, int) else pl.ds(pl.multiple_of(k * KB, KB), KB)
        if kind == 2:
            src = dst = rows_all.at[rows_of(over), cols]
        else:
            src, dst = own.at[:, cols], rows_all.at[rows_of(me), cols]
        return pltpu.make_async_remote_copy(src_ref=src, dst_ref=dst, send_sem=d_send.at[kind, k], recv_sem=d_recv.at[kind, k],
                                            device_id={'ep': over if kind == 0 else sib}, device_id_type=MESH)

    def disp_arrival(kind, k):
        cols = pl.ds(pl.multiple_of(k * KB, KB), KB)
        dst = rows_all.at[rows_of((over, sib, diag)[kind]), cols]
        return pltpu.make_async_remote_copy(src_ref=dst, dst_ref=dst, send_sem=d_send.at[kind, k], recv_sem=d_recv.at[kind, k],
                                            device_id={'ep': over if kind == 0 else sib}, device_id_type=MESH)

    for j in range(3):
        for what in range(2):
            idx_copy(j, what).start()
    own_copy.wait()
    for k in range(n_kb):
        disp_copy(0, k).start()
        disp_copy(1, k).start()

    for j in range(3):
        for what in range(2):
            idx_copy(j, what).wait()

    expert = lax.broadcasted_iota(jnp.int32, (n_exp, tok_dev), 0) + me * n_exp

    def side(src, ids_ref, gts_ref):
        ids, gts = ids_ref[...], gts_ref[...]
        hit_any = jnp.zeros((n_exp, tok_dev), jnp.int32)
        gate = jnp.zeros((n_exp, tok_dev), F32)
        for j in range(ids.shape[0]):
            hit = ids[j:j + 1, :] == expert
            hit_any = hit_any + jnp.where(hit, 1, 0)
            gate = gate + jnp.where(hit, gts[j:j + 1, :], 0.0)
        return hit_any, gate

    parts = {'me': side(None, ids_in, gts_in)}
    for j, name in enumerate(('over', 'diag', 'sib')):
        parts[name] = side(None, ids_all.at[j], gts_all.at[j])

    def pick_part(b, i):
        return jnp.where(me == b, parts['me'][i], jnp.where(over == b, parts['over'][i], jnp.where(diag == b, parts['diag'][i], parts['sib'][i])))

    member = jnp.concatenate([pick_part(b, 0) for b in range(GROUPS)], axis=1)
    gate = jnp.concatenate([pick_part(b, 1) for b in range(GROUPS)], axis=1)
    lane = lax.broadcasted_iota(jnp.int32, (n_exp, n_tok), 1)
    count = member
    shift = 1
    while shift < n_tok:
        count = count + jnp.where(lane >= shift, pltpu.roll(count, shift, 1), 0)
        shift *= 2
    is_mem = member > 0
    slot = jnp.where(is_mem, count - 1, -1)
    slots[...] = slot
    pos = lax.broadcasted_iota(jnp.int32, (n_exp, n_tok), 0) * CAP + slot
    big = n_exp * CAP
    pos1 = jnp.min(jnp.where(is_mem, pos, big), axis=0, keepdims=True)
    pos2 = jnp.max(jnp.where(is_mem, pos, -1), axis=0, keepdims=True)
    g1 = jnp.sum(jnp.where(is_mem & (pos == pos1), gate, 0.0), axis=0, keepdims=True)
    g2 = jnp.sum(jnp.where(is_mem & (pos == pos2), gate, 0.0), axis=0, keepdims=True)
    sub = lax.broadcasted_iota(jnp.int32, (8, n_tok), 0)
    packed = jnp.where(sub == 0, pos1.astype(F32), jnp.where(sub == 1, pos2.astype(F32), jnp.where(sub == 2, g1, jnp.where(sub == 3, g2, 0.0))))
    tbl[...] = jnp.transpose(packed)

    def build_picks(i, c):
        r = pl.ds(pl.multiple_of(i * 128, 128), 128)
        at = lax.broadcasted_iota(jnp.int32, (128, big), 1).astype(F32)
        pick1[r, :] = jnp.where(tbl[r, 0:1] == at, 1.0, 0.0).astype(BF16)
        pick2[r, :] = jnp.where(tbl[r, 1:2] == at, 1.0, 0.0).astype(BF16)
        return c

    lax.fori_loop(0, n_tok // 128, build_picks, 0)
    mine_copy.wait()

    def fan(e, k, par):
        cols = pl.ds(k * KB, KB)
        hot = lax.broadcasted_iota(jnp.int32, (CAP, n_tok), 0) == slots[pl.ds(e, 1), :]
        hot = jnp.where(hot, 1.0, 0.0).astype(BF16)
        xbuf[par] = jnp.dot(hot, rows_all[:, cols], preferred_element_type=F32).astype(BF16)

    disp_arrival(0, 0).wait_recv()
    disp_copy(2, 0).start()
    for k in range(n_kb):
        disp_arrival(1, k).wait_recv()
        disp_arrival(2, k).wait_recv()
        fan(0, k, 0)

        def step1(e, c, k=k):
            step = k * n_exp + e
            ring = lax.rem(step, RING1)
            par = lax.rem(e, 2)
            for copy in w1_copies(step, ring):
                copy.wait()
            x = xbuf[par]
            r = pl.ds(pl.multiple_of(e * CAP, CAP), CAP)
            gate_act = jnp.dot(x, ring1[ring, 0], preferred_element_type=F32)
            up_act = jnp.dot(x, ring1[ring, 1], preferred_element_type=F32)
            fan(lax.rem(e + 1, n_exp), k, 1 - par)
            if k > 0:
                gate_act = acc[r, :ffn] + gate_act
                up_act = acc[r, ffn:] + up_act
            if k < n_kb - 1:
                acc[r, :ffn] = gate_act
                acc[r, ffn:] = up_act
            else:
                hid[r, :] = (jax.nn.silu(gate_act) * up_act).astype(BF16)

            @pl.when(step + RING1 < steps1)
            def _():
                for copy in w1_copies(step + RING1, ring):
                    copy.start()

            if k < n_kb - 1:
                @pl.when(e == n_exp - 5)
                def _():
                    disp_arrival(0, k + 1).wait_recv()
                    disp_copy(2, k + 1).start()
            return c

        lax.fori_loop(0, n_exp, step1, 0)

    for k in range(n_kb):
        for kind in range(3):
            disp_copy(kind, k).wait_send()

    def ret_copy(j, d):
        cols = pl.ds(pl.multiple_of(d * DB, DB), DB)
        return pltpu.make_async_remote_copy(src_ref=rows_all.at[rows_of(peers[j]), cols], dst_ref=back.at[j, :, cols],
                                            send_sem=r_send.at[j, d], recv_sem=r_recv.at[j, d], device_id={'ep': peers[j]}, device_id_type=MESH)

    def block2(d, c):
        cols = pl.ds(pl.multiple_of(d * DB, DB), DB)

        def step2(g, c2):
            step = d * n_grp + g
            ring = lax.rem(step, RING2)
            w2_copy(step, ring).wait()
            for i in range(EPS):
                r = pl.ds(pl.multiple_of((g * EPS + i) * CAP, CAP), CAP)
                y_blk[r, :] = jnp.dot(hid[r, :], ring2[ring, i], preferred_element_type=F32).astype(BF16)

            @pl.when(step + RING2 < steps2)
            def _():
                w2_copy(step + RING2, ring).start()
            return c2

        lax.fori_loop(0, n_grp, step2, 0)

        for j, dev in enumerate((*peers, me)):
            r = rows_of(dev)
            y1 = jnp.dot(pick1[r, :], y_blk[...], preferred_element_type=F32)
            y2 = jnp.dot(pick2[r, :], y_blk[...], preferred_element_type=F32)
            rows_all[r, cols] = (tbl[r, 2:3] * y1 + tbl[r, 3:4] * y2).astype(BF16)
            if j < 3:
                ret_copy(j, d).start()
        return c

    lax.fori_loop(0, n_db, block2, 0)

    def out_copy(d):
        cols = pl.ds(pl.multiple_of(d * DB, DB), DB)
        return pltpu.make_async_copy(own.at[:, cols], out.at[:, cols], o_sem.at[d])

    def finish(d, c):
        cols = pl.ds(pl.multiple_of(d * DB, DB), DB)
        for j in range(3):
            ret_copy(j, d).wait_recv()
        total = own[:, cols].astype(F32) + rows_all[rows_of(me), cols].astype(F32)
        for j in range(3):
            total = total + back[j, :, cols].astype(F32)
        own[:, cols] = total.astype(BF16)
        out_copy(d).start()
        return c

    lax.fori_loop(0, n_db, finish, 0)

    def drain(d, c):
        for j in range(3):
            ret_copy(j, d).wait_send()
        out_copy(d).wait()
        return c

    lax.fori_loop(0, n_db, drain, 0)


def solution(mesh):
    row_spec = P(('dp', 'ep'))
    expert_spec = P('ep')

    def device_step(tokens, expert_ids, gate_vals, w_gate, w_up, w_down):
        tok_dev, d_model = tokens.shape
        n_exp, _, ffn = w_gate.shape
        top_k = expert_ids.shape[1]
        n_tok = GROUPS * tok_dev
        pairs = n_exp * CAP
        hbm = pl.BlockSpec(memory_space=pltpu.HBM)
        vmem = pl.BlockSpec(memory_space=pltpu.VMEM)
        dma = pltpu.SemaphoreType.DMA
        return pl.pallas_call(
            layer_kernel,
            out_shape=jax.ShapeDtypeStruct((tok_dev, d_model), BF16),
            in_specs=[hbm, vmem, vmem, hbm, hbm, hbm],
            out_specs=hbm,
            scratch_shapes=[
                pltpu.VMEM((pairs, 2 * ffn), F32),
                pltpu.VMEM((n_tok, d_model), BF16),
                pltpu.VMEM((tok_dev, d_model), BF16),
                pltpu.VMEM((pairs, ffn), BF16),
                pltpu.VMEM((RING1, 2, KB, ffn), BF16),
                pltpu.VMEM((RING2, EPS, ffn, DB), BF16),
                pltpu.VMEM((3, tok_dev, d_model), BF16),
                pltpu.VMEM((n_tok, pairs), BF16),
                pltpu.VMEM((n_tok, pairs), BF16),
                pltpu.VMEM((pairs, DB), BF16),
                pltpu.VMEM((2, CAP, KB), BF16),
                pltpu.VMEM((3, top_k, tok_dev), jnp.int32),
                pltpu.VMEM((3, top_k, tok_dev), F32),
                pltpu.VMEM((n_exp, n_tok), jnp.int32),
                pltpu.VMEM((n_tok, 8), F32),
                dma((RING1, 2)),
                dma((RING2,)),
                dma((2,)),
                dma((2, 3)),
                dma((2, 3)),
                dma((3, d_model // KB)),
                dma((3, d_model // KB)),
                dma((3, d_model // DB)),
                dma((3, d_model // DB)),
                dma((d_model // DB,)),
            ],
            compiler_params=pltpu.CompilerParams(collective_id=0, has_side_effects=True, vmem_limit_bytes=67043328),
        )(tokens, expert_ids.T, gate_vals.T, w_gate, w_up, w_down)

    return jax.shard_map(device_step, mesh=mesh, in_specs=(row_spec, row_spec, row_spec, expert_spec, expert_spec, expert_spec), out_specs=row_spec, check_vma=False)
```

time: 251 us -> 107 us (0.43)
  matrix products: 136 us -> 0 us
  Pallas kernels: 0 us -> 105 us
  blocking collectives: 50.8 us -> 0 us
  waiting for transfers between devices: 42.8 us -> 0 us
  other arithmetic: 10.1 us -> 0 us
  starting transfers between devices: 9.73 us -> 0 us
    dot_general x7 -> x0, matrix products: 136 us -> none  [the longest x1 31.7 us: expert_ffn(): jnp.einsum('lcf,lfd->lcd', hidden, w_down, preferred_element_type=jnp.flo...]
    pallas_call x0 -> x1, Pallas kernels: none -> 105 us  [device_step(): pl.pallas_call(layer_kernel, out_shape=jax.ShapeDtypeStruct((tok_dev, d_m...]
    all_to_all x1 -> x0, blocking collectives: 50.8 us -> none  [device_step(): lax.all_to_all(dev_sum.reshape(groups, pair_cap, d_model), 'ep', 0, 0, ti...]
    all_to_all x2 -> x0, waiting for transfers between devices: 42.8 us -> none  [the longest x1 42.8 us: device_step(): recv_rows = lax.all_to_all(send_rows, 'ep', 0, 0, tiled=True)]
    all_to_all x2 -> x0, starting transfers between devices: 9.73 us -> none  [the longest x1 5.12 us: device_step(): recv_rows = lax.all_to_all(send_rows, 'ep', 0, 0, tiled=True)]
    another operation x5 -> x0, other arithmetic: 5.81 us -> none
    reduce_sum x2 -> x0, other arithmetic: 3.01 us -> none  [the longest x1 2.24 us: send_tables(): jnp.sum(jnp.where(pack_mask[:, :, :, None], gate_t[:, None, :, :], 0.0),...]
  transfers between devices with their start and end apart: 2 -> 0, of which waited for: 1 -> 0; matrix products, arithmetic and copies ran while one was open for 4% -> 0% of each run, Pallas kernels for 0% -> 0%
where the time goes in v1:
time: 107 us
  Pallas kernels  105 us (98%)
  local copies, waits for them, and re-layouts  2.3 us (2%)
    pallas_call x1, Pallas kernels, device_step(): pl.pallas_call(layer_kernel, out_shape=jax.ShapeDtypeStruct((tok_dev, d_m...  105 us
    unnamed x1, local copies, waits for them, and re-layouts  2.3 us

profile of v1, /device:TPU:0, one launch (start us, length us, event | category | flops | bytes accessed | tf_op | source)
XLA Modules:
  0.0 107.0 jit_solution(7599952224243996967)
XLA Ops:
  0.0 104.7 %shard_map.64 = bf16[256,2048]{1,0:T(8,128)(2,1)} custom-call(bf16[256,2048]{1,0:T(8,128)(2,1)} %tok.1, s32[8,256]{1,0:T(8,128)} %bitcast.2, f32[8,256]{1,0:T(8,128)} %bitcast.3, bf16[16,2048,1024]{2,1,0:T(8,128)(2,1)} %w_gate.1, bf16[16,2048,1024]{2,1,0:T(8,128)(2,1)} %w_up.1, bf16[16,1024,2048]{2,1,0:T(8,128)(2,1)} %w_down.1), custom_call_target="tpu_custom_call" | custom-call | tf_op jit(solution)/shard_map/pallas_call | solution.py:279
  104.7 2.3 %copy.8 = bf16[256,2048]{1,0:T(8,128)(2,1)} copy(bf16[256,2048]{1,0:T(8,128)(2,1)} %shard_map.64) | data formatting | bytes 2097152

commit v2 on v1

--- a/solution.py
+++ b/solution.py
@@ -11,21 +11,29 @@
 F32, BF16 = jnp.float32, jnp.bfloat16
 GROUPS = 4
 CAP = 128
-KB = 512
+KU = 256
+BLOCKS = (1, 1, 2, 2, 2)
 DB = 256
 RING1 = 8
+PER_BODY = 2
 EPS = 4
 RING2 = 4
 
 
 def layer_kernel(tok, ids_in, gts_in, w_gate, w_up, w_down, out, acc, rows_all, own, hid, ring1, ring2, back, pick1, pick2,
-                 y_blk, xbuf, ids_all, gts_all, slots, tbl, w1_sem, w2_sem, loc_sem, idx_send, idx_recv, d_send, d_recv,
+                 y_blk, xbuf1, xbuf2, ids_all, gts_all, slots, tbl, w1_sem, w2_sem, loc_sem, idx_send, idx_recv, d_send, d_recv,
                  r_send, r_recv, o_sem):
     tok_dev, d_model = tok.shape
-    n_exp, _, ffn = w_gate.shape
+    n_exp, n_unit, _, ffn = w_gate.shape
     n_tok = GROUPS * tok_dev
-    n_kb, n_db, n_grp = d_model // KB, d_model // DB, n_exp // EPS
-    steps1, steps2 = n_kb * n_exp, n_db * n_grp
+    n_kb, n_db, n_grp = len(BLOCKS), d_model // DB, n_exp // EPS
+    firsts = [sum(BLOCKS[:k]) for k in range(n_kb)]
+    assert sum(BLOCKS) == n_unit
+    slot_exp = [2 // width for width in BLOCKS]
+    body_exp = [PER_BODY * m for m in slot_exp]
+    bodies = [n_exp // m for m in body_exp]
+    xbufs = {1: xbuf1, 2: xbuf2}
+    steps2 = n_db * n_grp
 
     me = lax.axis_index('ep')
     sib = me + 1 - 2 * lax.rem(me, 2)
@@ -36,11 +44,13 @@
     def rows_of(dev):
         return pl.ds(pl.multiple_of(dev * tok_dev, tok_dev), tok_dev)
 
-    def w1_copies(step, slot):
-        e, k = lax.rem(step, n_exp), lax.div(step, n_exp)
-        rows = pl.ds(pl.multiple_of(k * KB, KB), KB)
-        return (pltpu.make_async_copy(w_gate.at[e, rows, :], ring1.at[slot, 0], w1_sem.at[slot, 0]),
-                pltpu.make_async_copy(w_up.at[e, rows, :], ring1.at[slot, 1], w1_sem.at[slot, 1]))
+    def w1_copies(k, i, slot):
+        if BLOCKS[k] == 2:
+            part = (i, pl.ds(firsts[k], 2))
+        else:
+            part = (pl.ds(i * 2, 2), firsts[k])
+        return (pltpu.make_async_copy(w_gate.at[part], ring1.at[slot, 0], w1_sem.at[slot, 0]),
+                pltpu.make_async_copy(w_up.at[part], ring1.at[slot, 1], w1_sem.at[slot, 1]))
 
     def w2_copy(step, slot):
         g, d = lax.rem(step, n_grp), lax.div(step, n_grp)
@@ -53,7 +63,7 @@
     mine_copy.start()
 
     def prefetch1(step, c):
-        for copy in w1_copies(step, step):
+        for copy in w1_copies(0, step, step):
             copy.start()
         return c
 
@@ -76,7 +86,7 @@
                                             device_id={'ep': peers[j]}, device_id_type=MESH)
 
     def disp_copy(kind, k):
-        cols = pl.ds(k * KB, KB) if isinstance(k, int) else pl.ds(pl.multiple_of(k * KB, KB), KB)
+        cols = pl.ds(firsts[k] * KU, BLOCKS[k] * KU)
         if kind == 2:
             src = dst = rows_all.at[rows_of(over), cols]
         else:
@@ -85,7 +95,7 @@
                                             device_id={'ep': over if kind == 0 else sib}, device_id_type=MESH)
 
     def disp_arrival(kind, k):
-        cols = pl.ds(pl.multiple_of(k * KB, KB), KB)
+        cols = pl.ds(firsts[k] * KU, BLOCKS[k] * KU)
         dst = rows_all.at[rows_of((over, sib, diag)[kind]), cols]
         return pltpu.make_async_remote_copy(src_ref=dst, dst_ref=dst, send_sem=d_send.at[kind, k], recv_sem=d_recv.at[kind, k],
                                             device_id={'ep': over if kind == 0 else sib}, device_id_type=MESH)
@@ -152,52 +162,84 @@
     lax.fori_loop(0, n_tok // 128, build_picks, 0)
     mine_copy.wait()
 
-    def fan(e, k, par):
-        cols = pl.ds(k * KB, KB)
-        hot = lax.broadcasted_iota(jnp.int32, (CAP, n_tok), 0) == slots[pl.ds(e, 1), :]
-        hot = jnp.where(hot, 1.0, 0.0).astype(BF16)
-        xbuf[par] = jnp.dot(hot, rows_all[:, cols], preferred_element_type=F32).astype(BF16)
+    def fan(k, i, par):
+        cols = pl.ds(firsts[k] * KU, BLOCKS[k] * KU)
+        at = lax.broadcasted_iota(jnp.int32, (CAP, n_tok), 0)
+        hot = jnp.concatenate([jnp.where(at == slots[pl.ds(i * body_exp[k] + m, 1), :], 1.0, 0.0).astype(BF16) for m in range(body_exp[k])], axis=0)
+        xbufs[BLOCKS[k]][par] = jnp.dot(hot, rows_all[:, cols], preferred_element_type=F32).astype(BF16)
+
+    def body1(k, i, nxt):
+        par = lax.rem(i, 2) if not isinstance(i, int) else i % 2
+        base = sum(n_exp // slot_exp[j] for j in range(k)) + i * PER_BODY
+        rings = [lax.rem(base + m, RING1) if not isinstance(i, int) else (base + m) % RING1 for m in range(PER_BODY)]
+        for m in range(PER_BODY):
+            for copy in w1_copies(k, i * PER_BODY + m, rings[m]):
+                copy.wait()
+        x = xbufs[BLOCKS[k]].at[par]
+        for m in range(body_exp[k]):
+            ring, xr = rings[m // slot_exp[k]], pl.ds(m * CAP, CAP)
+            r = pl.ds(pl.multiple_of((i * body_exp[k] + m) * CAP, CAP), CAP)
+            acts = []
+            for p in range(2):
+                if BLOCKS[k] == 2:
+                    act = (jnp.dot(x[xr, :KU], ring1[ring, p, 0], preferred_element_type=F32) +
+                           jnp.dot(x[xr, KU:], ring1[ring, p, 1], preferred_element_type=F32))
+                else:
+                    act = jnp.dot(x[xr, :], ring1[ring, p, m % 2], preferred_element_type=F32)
+                if k > 0:
+                    act = acc[r, p * ffn:(p + 1) * ffn] + act
+                if k < n_kb - 1:
+                    acc[r, p * ffn:(p + 1) * ffn] = act
+                acts.append(act)
+            if k == n_kb - 1:
+                hid[r, :] = (jax.nn.silu(acts[0]) * acts[1]).astype(BF16)
+        if nxt is not None:
+            fan(*nxt, 1 - par)
+
+        for m in range(PER_BODY):
+            ahead, n_here = i * PER_BODY + m + RING1, n_exp // slot_exp[k]
+
+            def refill(kk, ii, m=m):
+                for copy in w1_copies(kk, ii, rings[m]):
+                    copy.start()
+
+            if isinstance(i, int):
+                if ahead < n_here:
+                    refill(k, ahead)
+                elif k < n_kb - 1:
+                    refill(k + 1, ahead - n_here)
+            elif n_here == RING1:
+                refill(k + 1, ahead - n_here)
+            else:
+                @pl.when(ahead < n_here)
+                def _():
+                    refill(k, ahead)
+
+                if k < n_kb - 1:
+                    @pl.when(ahead >= n_here)
+                    def _():
+                        refill(k + 1, ahead - n_here)
 
     disp_arrival(0, 0).wait_recv()
     disp_copy(2, 0).start()
+    disp_arrival(1, 0).wait_recv()
+    disp_arrival(2, 0).wait_recv()
+    fan(0, 0, 0)
     for k in range(n_kb):
-        disp_arrival(1, k).wait_recv()
-        disp_arrival(2, k).wait_recv()
-        fan(0, k, 0)
-
-        def step1(e, c, k=k):
-            step = k * n_exp + e
-            ring = lax.rem(step, RING1)
-            par = lax.rem(e, 2)
-            for copy in w1_copies(step, ring):
-                copy.wait()
-            x = xbuf[par]
-            r = pl.ds(pl.multiple_of(e * CAP, CAP), CAP)
-            gate_act = jnp.dot(x, ring1[ring, 0], preferred_element_type=F32)
-            up_act = jnp.dot(x, ring1[ring, 1], preferred_element_type=F32)
-            fan(lax.rem(e + 1, n_exp), k, 1 - par)
-            if k > 0:
-                gate_act = acc[r, :ffn] + gate_act
-                up_act = acc[r, ffn:] + up_act
+        def loop1(i, c, k=k):
+            body1(k, i, (k, i + 1))
             if k < n_kb - 1:
-                acc[r, :ffn] = gate_act
-                acc[r, ffn:] = up_act
-            else:
-                hid[r, :] = (jax.nn.silu(gate_act) * up_act).astype(BF16)
-
-            @pl.when(step + RING1 < steps1)
-            def _():
-                for copy in w1_copies(step + RING1, ring):
-                    copy.start()
-
-            if k < n_kb - 1:
-                @pl.when(e == n_exp - 5)
+                @pl.when(i == bodies[k] - 3)
                 def _():
                     disp_arrival(0, k + 1).wait_recv()
                     disp_copy(2, k + 1).start()
             return c
 
-        lax.fori_loop(0, n_exp, step1, 0)
+        lax.fori_loop(0, bodies[k] - 1, loop1, 0)
+        if k < n_kb - 1:
+            disp_arrival(1, k + 1).wait_recv()
+            disp_arrival(2, k + 1).wait_recv()
+        body1(k, bodies[k] - 1, (k + 1, 0) if k < n_kb - 1 else None)
 
     for k in range(n_kb):
         for kind in range(3):
@@ -273,6 +315,7 @@
         top_k = expert_ids.shape[1]
         n_tok = GROUPS * tok_dev
         pairs = n_exp * CAP
+        units = (n_exp, d_model // KU, KU, ffn)
         hbm = pl.BlockSpec(memory_space=pltpu.HBM)
         vmem = pl.BlockSpec(memory_space=pltpu.VMEM)
         dma = pltpu.SemaphoreType.DMA
@@ -286,13 +329,14 @@
                 pltpu.VMEM((n_tok, d_model), BF16),
                 pltpu.VMEM((tok_dev, d_model), BF16),
                 pltpu.VMEM((pairs, ffn), BF16),
-                pltpu.VMEM((RING1, 2, KB, ffn), BF16),
+                pltpu.VMEM((RING1, 2, 2, KU, ffn), BF16),
                 pltpu.VMEM((RING2, EPS, ffn, DB), BF16),
                 pltpu.VMEM((3, tok_dev, d_model), BF16),
                 pltpu.VMEM((n_tok, pairs), BF16),
                 pltpu.VMEM((n_tok, pairs), BF16),
                 pltpu.VMEM((pairs, DB), BF16),
-                pltpu.VMEM((2, CAP, KB), BF16),
+                pltpu.VMEM((2, 4 * CAP, KU), BF16),
+                pltpu.VMEM((2, 2 * CAP, 2 * KU), BF16),
                 pltpu.VMEM((3, top_k, tok_dev), jnp.int32),
                 pltpu.VMEM((3, top_k, tok_dev), F32),
                 pltpu.VMEM((n_exp, n_tok), jnp.int32),
@@ -302,13 +346,13 @@
                 dma((2,)),
                 dma((2, 3)),
                 dma((2, 3)),
-                dma((3, d_model // KB)),
-                dma((3, d_model // KB)),
+                dma((3, len(BLOCKS))),
+                dma((3, len(BLOCKS))),
                 dma((3, d_model // DB)),
                 dma((3, d_model // DB)),
                 dma((d_model // DB,)),
             ],
             compiler_params=pltpu.CompilerParams(collective_id=0, has_side_effects=True, vmem_limit_bytes=67043328),
-        )(tokens, expert_ids.T, gate_vals.T, w_gate, w_up, w_down)
+        )(tokens, expert_ids.T, gate_vals.T, w_gate.reshape(units), w_up.reshape(units), w_down)
 
     return jax.shard_map(device_step, mesh=mesh, in_specs=(row_spec, row_spec, row_spec, expert_spec, expert_spec, expert_spec), out_specs=row_spec, check_vma=False)

time: 107 us -> 102 us (0.953)
  Pallas kernels: 105 us -> 99.3 us
    pallas_call x1, Pallas kernels: 105 us -> 99.3 us  [device_step(): pl.pallas_call(layer_kernel, out_shape=jax.ShapeDtypeStruct((tok_dev, d_m...]
where the time goes in v2:
time: 102 us
  Pallas kernels  99.3 us (97%)
  local copies, waits for them, and re-layouts  2.3 us (2%)
    pallas_call x1, Pallas kernels, device_step(): pl.pallas_call(layer_kernel, out_shape=jax.ShapeDtypeStruct((tok_dev, d_m...  99.3 us
    unnamed x1, local copies, waits for them, and re-layouts  2.3 us

profile of v2, /device:TPU:0, one launch (start us, length us, event | category | flops | bytes accessed | tf_op | source)
XLA Modules:
  0.0 101.6 jit_solution(7088607363500199841)
XLA Ops:
  0.0 99.3 %shard_map.64 = bf16[256,2048]{1,0:T(8,128)(2,1)} custom-call(bf16[256,2048]{1,0:T(8,128)(2,1)} %tok.1, s32[8,256]{1,0:T(8,128)} %bitcast.4, f32[8,256]{1,0:T(8,128)} %bitcast.5, bf16[16,8,256,1024]{3,2,1,0:T(8,128)(2,1)} %bitcast.2.w_gate, bf16[16,8,256,1024]{3,2,1,0:T(8,128)(2,1)} %bitcast.3.w_up, bf16[16,1024,2048]{2,1,0:T(8,128)(2,1)} %w_down.1), custom_call_target="tpu_custom_call" | custom-call | tf_op jit(solution)/shard_map/pallas_call | solution.py:322
  99.3 2.3 %copy.8 = bf16[256,2048]{1,0:T(8,128)(2,1)} copy(bf16[256,2048]{1,0:T(8,128)(2,1)} %shard_map.64) | data formatting | bytes 2097152

commit v3 on v2

--- a/solution.py
+++ b/solution.py
@@ -1,5 +1,3 @@
-import functools
-
 import jax
 import jax.numpy as jnp
 from jax import lax
@@ -15,24 +13,25 @@
 BLOCKS = (1, 1, 2, 2, 2)
 DB = 256
 RING1 = 8
+EXTRA = 4
 PER_BODY = 2
 EPS = 4
 RING2 = 4
 
 
-def layer_kernel(tok, ids_in, gts_in, w_gate, w_up, w_down, out, acc, rows_all, own, hid, ring1, ring2, back, pick1, pick2,
-                 y_blk, xbuf1, xbuf2, ids_all, gts_all, slots, tbl, w1_sem, w2_sem, loc_sem, idx_send, idx_recv, d_send, d_recv,
+def layer_kernel(tok, ids_in, gts_in, w_gate, w_up, w_down, out, acc, rows_all, own, hid, ring1, ring2, back,
+                 y_blk, xbuf, ids_all, gts_all, slots, tbl, w1_sem, w2_sem, loc_sem, idx_send, idx_recv, d_send, d_recv,
                  r_send, r_recv, o_sem):
     tok_dev, d_model = tok.shape
     n_exp, n_unit, _, ffn = w_gate.shape
     n_tok = GROUPS * tok_dev
     n_kb, n_db, n_grp = len(BLOCKS), d_model // DB, n_exp // EPS
     firsts = [sum(BLOCKS[:k]) for k in range(n_kb)]
-    assert sum(BLOCKS) == n_unit
+    assert sum(BLOCKS) == n_unit and BLOCKS[:3] == (1, 1, 2) and set(BLOCKS[2:]) == {2} and n_exp == GROUPS * EPS
     slot_exp = [2 // width for width in BLOCKS]
     body_exp = [PER_BODY * m for m in slot_exp]
     bodies = [n_exp // m for m in body_exp]
-    xbufs = {1: xbuf1, 2: xbuf2}
+    bases = [sum(n_exp // m for m in slot_exp[:k]) for k in range(n_kb + 1)]
     steps2 = n_db * n_grp
 
     me = lax.axis_index('ep')
@@ -52,6 +51,13 @@
         return (pltpu.make_async_copy(w_gate.at[part], ring1.at[slot, 0], w1_sem.at[slot, 0]),
                 pltpu.make_async_copy(w_up.at[part], ring1.at[slot, 1], w1_sem.at[slot, 1]))
 
+    def ring_slot(k, s):
+        if k == 0:
+            return s
+        if k == 1:
+            return s % (RING1 + EXTRA)
+        return lax.rem(s + RING1 - EXTRA, RING1) if not isinstance(s, int) else (s + RING1 - EXTRA) % RING1
+
     def w2_copy(step, slot):
         g, d = lax.rem(step, n_grp), lax.div(step, n_grp)
         cols = pl.ds(pl.multiple_of(d * DB, DB), DB)
@@ -60,24 +66,13 @@
     own_copy = pltpu.make_async_copy(tok, own, loc_sem.at[0])
     mine_copy = pltpu.make_async_copy(tok, rows_all.at[rows_of(me), :], loc_sem.at[1])
     own_copy.start()
-    mine_copy.start()
-
-    def prefetch1(step, c):
-        for copy in w1_copies(0, step, step):
-            copy.start()
-        return c
-
-    lax.fori_loop(0, RING1, prefetch1, 0)
-
-    def prefetch2(step, c):
-        w2_copy(step, step).start()
-        return c
-
-    lax.fori_loop(0, RING2, prefetch2, 0)
-
     barrier = pltpu.get_barrier_semaphore()
     for dev in peers:
         pl.semaphore_signal(barrier, inc=1, device_id={'ep': dev}, device_id_type=MESH)
+    mine_copy.start()
+    for s in range(RING1):
+        for copy in w1_copies(0, s, s):
+            copy.start()
     pl.semaphore_wait(barrier, len(peers))
 
     def idx_copy(j, what):
@@ -107,6 +102,11 @@
     for k in range(n_kb):
         disp_copy(0, k).start()
         disp_copy(1, k).start()
+    for s in range(EXTRA):
+        for copy in w1_copies(1, s, RING1 + s):
+            copy.start()
+    for s in range(RING2):
+        w2_copy(s, s).start()
 
     for j in range(3):
         for what in range(2):
@@ -114,7 +114,7 @@
 
     expert = lax.broadcasted_iota(jnp.int32, (n_exp, tok_dev), 0) + me * n_exp
 
-    def side(src, ids_ref, gts_ref):
+    def side(ids_ref, gts_ref):
         ids, gts = ids_ref[...], gts_ref[...]
         hit_any = jnp.zeros((n_exp, tok_dev), jnp.int32)
         gate = jnp.zeros((n_exp, tok_dev), F32)
@@ -124,15 +124,14 @@
             gate = gate + jnp.where(hit, gts[j:j + 1, :], 0.0)
         return hit_any, gate
 
-    parts = {'me': side(None, ids_in, gts_in)}
-    for j, name in enumerate(('over', 'diag', 'sib')):
-        parts[name] = side(None, ids_all.at[j], gts_all.at[j])
-
-    def pick_part(b, i):
-        return jnp.where(me == b, parts['me'][i], jnp.where(over == b, parts['over'][i], jnp.where(diag == b, parts['diag'][i], parts['sib'][i])))
-
-    member = jnp.concatenate([pick_part(b, 0) for b in range(GROUPS)], axis=1)
-    gate = jnp.concatenate([pick_part(b, 1) for b in range(GROUPS)], axis=1)
+    parts = [side(ids_in, gts_in)] + [side(ids_all.at[j], gts_all.at[j]) for j in range(3)]
+
+    def of_device(b, i):
+        p = [part[i] for part in parts]
+        return jnp.where(me == b, p[0], jnp.where(over == b, p[1], jnp.where(diag == b, p[2], p[3])))
+
+    member = jnp.concatenate([of_device(b, 0) for b in range(GROUPS)], axis=1)
+    gate = jnp.concatenate([of_device(b, 1) for b in range(GROUPS)], axis=1)
     lane = lax.broadcasted_iota(jnp.int32, (n_exp, n_tok), 1)
     count = member
     shift = 1
@@ -151,41 +150,55 @@
     sub = lax.broadcasted_iota(jnp.int32, (8, n_tok), 0)
     packed = jnp.where(sub == 0, pos1.astype(F32), jnp.where(sub == 1, pos2.astype(F32), jnp.where(sub == 2, g1, jnp.where(sub == 3, g2, 0.0))))
     tbl[...] = jnp.transpose(packed)
-
-    def build_picks(i, c):
-        r = pl.ds(pl.multiple_of(i * 128, 128), 128)
-        at = lax.broadcasted_iota(jnp.int32, (128, big), 1).astype(F32)
-        pick1[r, :] = jnp.where(tbl[r, 0:1] == at, 1.0, 0.0).astype(BF16)
-        pick2[r, :] = jnp.where(tbl[r, 1:2] == at, 1.0, 0.0).astype(BF16)
-        return c
-
-    lax.fori_loop(0, n_tok // 128, build_picks, 0)
     mine_copy.wait()
+
+    half = big // 2
+    pick_rows = n_tok // 8
+
+    def build_picks(i):
+        dev, r = i // 2, (i % 2) * pick_rows
+        if not isinstance(i, int):
+            dev, r = lax.div(i, 2), pl.multiple_of(lax.rem(i, 2) * pick_rows, pick_rows)
+        t = tbl[pl.ds(i * pick_rows, pick_rows), :]
+        for h in range(2):
+            at = (lax.broadcasted_iota(jnp.int32, (pick_rows, half), 1) + h * half).astype(F32)
+            for p in range(2):
+                ring1[RING1 + dev, h, p, pl.ds(r, pick_rows), :] = jnp.where(t[:, p:p + 1] == at, 1.0, 0.0).astype(BF16)
 
     def fan(k, i, par):
         cols = pl.ds(firsts[k] * KU, BLOCKS[k] * KU)
         at = lax.broadcasted_iota(jnp.int32, (CAP, n_tok), 0)
         hot = jnp.concatenate([jnp.where(at == slots[pl.ds(i * body_exp[k] + m, 1), :], 1.0, 0.0).astype(BF16) for m in range(body_exp[k])], axis=0)
-        xbufs[BLOCKS[k]][par] = jnp.dot(hot, rows_all[:, cols], preferred_element_type=F32).astype(BF16)
-
-    def body1(k, i, nxt):
-        par = lax.rem(i, 2) if not isinstance(i, int) else i % 2
-        base = sum(n_exp // slot_exp[j] for j in range(k)) + i * PER_BODY
-        rings = [lax.rem(base + m, RING1) if not isinstance(i, int) else (base + m) % RING1 for m in range(PER_BODY)]
+        x = jnp.dot(hot, rows_all[:, cols], preferred_element_type=F32).astype(BF16)
+        for u in range(2):
+            if BLOCKS[k] == 2:
+                xbuf[par, u] = x[:, u * KU:(u + 1) * KU]
+            else:
+                xbuf[par, u] = x[u * 2 * CAP:(u + 1) * 2 * CAP, :]
+
+    def down(e, ring):
+        r = pl.ds(pl.multiple_of(e * CAP, CAP), CAP)
+        y_blk[r, :] = jnp.dot(hid[r, :], ring2[ring, e % EPS if isinstance(e, int) else lax.rem(e, EPS)], preferred_element_type=F32).astype(BF16)
+
+    def body1(k, i, nxt, last_of=None):
+        static = isinstance(i, int)
+        par = i % 2 if static else lax.rem(i, 2)
+        steps = [bases[k] + i * PER_BODY + m for m in range(PER_BODY)]
+        rings = [ring_slot(k, s) for s in steps]
         for m in range(PER_BODY):
             for copy in w1_copies(k, i * PER_BODY + m, rings[m]):
                 copy.wait()
-        x = xbufs[BLOCKS[k]].at[par]
         for m in range(body_exp[k]):
-            ring, xr = rings[m // slot_exp[k]], pl.ds(m * CAP, CAP)
+            ring = rings[m // slot_exp[k]]
             r = pl.ds(pl.multiple_of((i * body_exp[k] + m) * CAP, CAP), CAP)
             acts = []
             for p in range(2):
                 if BLOCKS[k] == 2:
-                    act = (jnp.dot(x[xr, :KU], ring1[ring, p, 0], preferred_element_type=F32) +
-                           jnp.dot(x[xr, KU:], ring1[ring, p, 1], preferred_element_type=F32))
+                    xr = pl.ds(m * CAP, CAP)
+                    act = (jnp.dot(xbuf[par, 0, xr, :], ring1[ring, p, 0], preferred_element_type=F32) +
+                           jnp.dot(xbuf[par, 1, xr, :], ring1[ring, p, 1], preferred_element_type=F32))
                 else:
-                    act = jnp.dot(x[xr, :], ring1[ring, p, m % 2], preferred_element_type=F32)
+                    act = jnp.dot(xbuf[par, m // 2, pl.ds((m % 2) * CAP, CAP), :], ring1[ring, p, m % 2], preferred_element_type=F32)
                 if k > 0:
                     act = acc[r, p * ffn:(p + 1) * ffn] + act
                 if k < n_kb - 1:
@@ -195,30 +208,36 @@
                 hid[r, :] = (jax.nn.silu(acts[0]) * acts[1]).astype(BF16)
         if nxt is not None:
             fan(*nxt, 1 - par)
+        if k == 2:
+            build_picks(i)
+        if last_of is not None:
+            for m in range(body_exp[k]):
+                e = last_of * body_exp[k] + m
+                down(e, e // EPS if isinstance(e, int) else lax.div(e, EPS))
 
         for m in range(PER_BODY):
-            ahead, n_here = i * PER_BODY + m + RING1, n_exp // slot_exp[k]
-
-            def refill(kk, ii, m=m):
-                for copy in w1_copies(kk, ii, rings[m]):
+            def refill(s):
+                kk = max(j for j in range(n_kb) if bases[j] <= s)
+                for copy in w1_copies(kk, s - bases[kk], rings[m]):
                     copy.start()
 
-            if isinstance(i, int):
-                if ahead < n_here:
-                    refill(k, ahead)
-                elif k < n_kb - 1:
-                    refill(k + 1, ahead - n_here)
-            elif n_here == RING1:
-                refill(k + 1, ahead - n_here)
+            if static:
+                ahead = steps[m] + RING1 + (EXTRA if steps[m] < RING1 else 0)
+                if ahead < bases[n_kb] and not RING1 <= steps[m] < RING1 + EXTRA:
+                    refill(ahead)
             else:
-                @pl.when(ahead < n_here)
+                ii, n_here = i * PER_BODY + m + RING1, n_exp // slot_exp[k]
+
+                @pl.when(ii < n_here)
                 def _():
-                    refill(k, ahead)
+                    for copy in w1_copies(k, ii, rings[m]):
+                        copy.start()
 
                 if k < n_kb - 1:
-                    @pl.when(ahead >= n_here)
+                    @pl.when(ii >= n_here)
                     def _():
-                        refill(k + 1, ahead - n_here)
+                        for copy in w1_copies(k + 1, ii - n_here, rings[m]):
+                            copy.start()
 
     disp_arrival(0, 0).wait_recv()
     disp_copy(2, 0).start()
@@ -226,20 +245,43 @@
     disp_arrival(2, 0).wait_recv()
     fan(0, 0, 0)
     for k in range(n_kb):
-        def loop1(i, c, k=k):
-            body1(k, i, (k, i + 1))
-            if k < n_kb - 1:
-                @pl.when(i == bodies[k] - 3)
-                def _():
-                    disp_arrival(0, k + 1).wait_recv()
-                    disp_copy(2, k + 1).start()
+        last, n_body = k == n_kb - 1, bodies[k]
+
+        def hand_on(k=k):
+            disp_arrival(0, k + 1).wait_recv()
+            disp_copy(2, k + 1).start()
+
+        def loop1(i, c, k=k, last=last, n_body=n_body, hand_on=hand_on):
+            body1(k, i, (k, i + 1), i - 1 if last else None)
+            if not last:
+                pl.when(i == n_body - 3)(hand_on)
             return c
 
-        lax.fori_loop(0, bodies[k] - 1, loop1, 0)
-        if k < n_kb - 1:
+        if k < 2:
+            for i in range(n_body - 1):
+                body1(k, i, (k, i + 1))
+                if i == n_body - 3:
+                    hand_on()
+        elif last:
+            for g in range(RING2):
+                w2_copy(g, g).wait()
+            body1(k, 0, (k, 1))
+            lax.fori_loop(1, n_body - 1, loop1, 0)
+        else:
+            lax.fori_loop(0, n_body - 1, loop1, 0)
+        if not last:
             disp_arrival(1, k + 1).wait_recv()
             disp_arrival(2, k + 1).wait_recv()
-        body1(k, bodies[k] - 1, (k + 1, 0) if k < n_kb - 1 else None)
+        body1(k, n_body - 1, None if last else (k + 1, 0), n_body - 2 if last else None)
+
+    for m in range(body_exp[-1]):
+        down(n_exp - body_exp[-1] + m, n_grp - 1)
+
+    def refill2(g, c):
+        w2_copy(n_grp + g, g).start()
+        return c
+
+    lax.fori_loop(0, RING2, refill2, 0)
 
     for k in range(n_kb):
         for kind in range(3):
@@ -250,9 +292,18 @@
         return pltpu.make_async_remote_copy(src_ref=rows_all.at[rows_of(peers[j]), cols], dst_ref=back.at[j, :, cols],
                                             send_sem=r_send.at[j, d], recv_sem=r_recv.at[j, d], device_id={'ep': peers[j]}, device_id_type=MESH)
 
+    def combine(d):
+        cols = pl.ds(pl.multiple_of(d * DB, DB), DB)
+        for j, dev in enumerate((*peers, me)):
+            r = rows_of(dev)
+            y12 = sum(jnp.dot(ring1[RING1 + dev, h].reshape(2 * tok_dev, half), y_blk[h * half:(h + 1) * half, :], preferred_element_type=F32) for h in range(2))
+            rows_all[r, cols] = (tbl[r, 2:3] * y12[:tok_dev] + tbl[r, 3:4] * y12[tok_dev:]).astype(BF16)
+            if j < 3:
+                ret_copy(j, d).start()
+
+    combine(0)
+
     def block2(d, c):
-        cols = pl.ds(pl.multiple_of(d * DB, DB), DB)
-
         def step2(g, c2):
             step = d * n_grp + g
             ring = lax.rem(step, RING2)
@@ -267,17 +318,10 @@
             return c2
 
         lax.fori_loop(0, n_grp, step2, 0)
-
-        for j, dev in enumerate((*peers, me)):
-            r = rows_of(dev)
-            y1 = jnp.dot(pick1[r, :], y_blk[...], preferred_element_type=F32)
-            y2 = jnp.dot(pick2[r, :], y_blk[...], preferred_element_type=F32)
-            rows_all[r, cols] = (tbl[r, 2:3] * y1 + tbl[r, 3:4] * y2).astype(BF16)
-            if j < 3:
-                ret_copy(j, d).start()
+        combine(d)
         return c
 
-    lax.fori_loop(0, n_db, block2, 0)
+    lax.fori_loop(1, n_db, block2, 0)
 
     def out_copy(d):
         cols = pl.ds(pl.multiple_of(d * DB, DB), DB)
@@ -329,19 +373,16 @@
                 pltpu.VMEM((n_tok, d_model), BF16),
                 pltpu.VMEM((tok_dev, d_model), BF16),
                 pltpu.VMEM((pairs, ffn), BF16),
-                pltpu.VMEM((RING1, 2, 2, KU, ffn), BF16),
+                pltpu.VMEM((RING1 + EXTRA, 2, 2, KU, ffn), BF16),
                 pltpu.VMEM((RING2, EPS, ffn, DB), BF16),
                 pltpu.VMEM((3, tok_dev, d_model), BF16),
-                pltpu.VMEM((n_tok, pairs), BF16),
-                pltpu.VMEM((n_tok, pairs), BF16),
                 pltpu.VMEM((pairs, DB), BF16),
-                pltpu.VMEM((2, 4 * CAP, KU), BF16),
-                pltpu.VMEM((2, 2 * CAP, 2 * KU), BF16),
+                pltpu.VMEM((2, 2, 2 * CAP, KU), BF16),
                 pltpu.VMEM((3, top_k, tok_dev), jnp.int32),
                 pltpu.VMEM((3, top_k, tok_dev), F32),
                 pltpu.VMEM((n_exp, n_tok), jnp.int32),
                 pltpu.VMEM((n_tok, 8), F32),
-                dma((RING1, 2)),
+                dma((RING1 + EXTRA, 2)),
                 dma((RING2,)),
                 dma((2,)),
                 dma((2, 3)),

time: 102 us -> 112 us (1.098)
  Pallas kernels: 99.3 us -> 110 us
    pallas_call x1, Pallas kernels: 99.3 us -> 110 us  [device_step(): pl.pallas_call(layer_kernel, out_shape=jax.ShapeDtypeStruct((tok_dev, d_m...]
where the time goes in v3:
time: 112 us
  Pallas kernels  110 us (98%)
  local copies, waits for them, and re-layouts  2.3 us (2%)
    pallas_call x1, Pallas kernels, device_step(): pl.pallas_call(layer_kernel, out_shape=jax.ShapeDtypeStruct((tok_dev, d_m...  110 us
    unnamed x1, local copies, waits for them, and re-layouts  2.3 us

profile of v3, /device:TPU:0, one launch (start us, length us, event | category | flops | bytes accessed | tf_op | source)
XLA Modules:
  0.0 112.2 jit_solution(7738099852439560326)
XLA Ops:
  0.0 109.9 %shard_map.64 = bf16[256,2048]{1,0:T(8,128)(2,1)} custom-call(bf16[256,2048]{1,0:T(8,128)(2,1)} %tok.1, s32[8,256]{1,0:T(8,128)} %bitcast.4, f32[8,256]{1,0:T(8,128)} %bitcast.5, bf16[16,8,256,1024]{3,2,1,0:T(8,128)(2,1)} %bitcast.2.w_gate, bf16[16,8,256,1024]{3,2,1,0:T(8,128)(2,1)} %bitcast.3.w_up, bf16[16,1024,2048]{2,1,0:T(8,128)(2,1)} %w_down.1), custom_call_target="tpu_custom_call" | custom-call | tf_op jit(solution)/shard_map/pallas_call | solution.py:366
  109.9 2.3 %copy.8 = bf16[256,2048]{1,0:T(8,128)(2,1)} copy(bf16[256,2048]{1,0:T(8,128)(2,1)} %shard_map.64) | data formatting | bytes 2097152

commit v4 on v1

v4 whole, which is shorter than its diff:
```python
import jax
import jax.numpy as jnp
from jax import lax
from jax.experimental import pallas as pl
from jax.experimental.pallas import tpu as pltpu
from jax.sharding import PartitionSpec as P

MESH = pl.DeviceIdType.MESH
F32, BF16 = jnp.float32, jnp.bfloat16
GROUPS = 4
CAP = 128
KU = 256
DB = 256
RING1 = 8
EXTRA = 4
PER_BODY = 2
EPS = 4
RING2 = 4


def layer_kernel(tok, ids_in, gts_in, w_gate, w_up, w_down, out, acc, rows_all, hid, ring1, ring2, back,
                 y_blk, xbuf, ids_all, gts_all, slots, tbl, w1_sem, w2_sem, loc_sem, idx_send, idx_recv, d_send, d_recv,
                 r_send, r_recv, o_sem):
    tok_dev, d_model = tok.shape
    n_exp, n_unit, _, ffn = w_gate.shape
    n_tok = GROUPS * tok_dev
    n_kb, n_db, n_grp = 2 + (n_unit - 2) // 2, d_model // DB, n_exp // EPS
    n_one, n_two = n_exp // 4, n_exp // 2
    steps2 = n_db * n_grp

    me = lax.axis_index('ep')
    sib = me + 1 - 2 * lax.rem(me, 2)
    over = lax.rem(me + 2, GROUPS)
    diag = lax.rem(sib + 2, GROUPS)
    peers = (over, diag, sib)

    def rows_of(dev):
        return pl.ds(pl.multiple_of(dev * tok_dev, tok_dev), tok_dev)

    def first_unit(k):
        return k if isinstance(k, int) and k < 2 else 2 * k - 2

    def w1_copies(k, i, slot):
        if isinstance(k, int) and k < 2:
            part = (pl.ds(i * 2, 2), k)
        else:
            part = (i, pl.ds(first_unit(k), 2))
        return (pltpu.make_async_copy(w_gate.at[part], ring1.at[slot, 0], w1_sem.at[slot, 0]),
                pltpu.make_async_copy(w_up.at[part], ring1.at[slot, 1], w1_sem.at[slot, 1]))

    def block_cols(k):
        if isinstance(k, int):
            return pl.ds(first_unit(k) * KU, KU if k < 2 else 2 * KU)
        return pl.ds(pl.multiple_of(first_unit(k) * KU, 2 * KU), 2 * KU)

    def w2_copy(step, slot):
        g, d = lax.rem(step, n_grp), lax.div(step, n_grp)
        cols = pl.ds(pl.multiple_of(d * DB, DB), DB)
        return pltpu.make_async_copy(w_down.at[pl.ds(g * EPS, EPS), :, cols], ring2.at[slot], w2_sem.at[slot])

    mine_copy = pltpu.make_async_copy(tok, rows_all.at[rows_of(me), :], loc_sem.at[0])
    mine_copy.start()
    barrier = pltpu.get_barrier_semaphore()
    for dev in peers:
        pl.semaphore_signal(barrier, inc=1, device_id={'ep': dev}, device_id_type=MESH)

    def start0(i, c):
        for copy in w1_copies(0, i, i):
            copy.start()
        return c

    lax.fori_loop(0, RING1, start0, 0)
    pl.semaphore_wait(barrier, len(peers))

    def idx_copy(j, what):
        src, dst = (ids_in, ids_all) if what == 0 else (gts_in, gts_all)
        return pltpu.make_async_remote_copy(src_ref=src, dst_ref=dst.at[j], send_sem=idx_send.at[what, j], recv_sem=idx_recv.at[what, j],
                                            device_id={'ep': peers[j]}, device_id_type=MESH)

    def disp_copy(kind, k):
        cols = block_cols(k)
        rows = rows_all.at[rows_of(over if kind == 2 else me), cols]
        return pltpu.make_async_remote_copy(src_ref=rows, dst_ref=rows, send_sem=d_send.at[kind, k], recv_sem=d_recv.at[kind, k],
                                            device_id={'ep': over if kind == 0 else sib}, device_id_type=MESH)

    def disp_arrival(kind, k):
        cols = block_cols(k)
        dst = rows_all.at[rows_of((over, sib, diag)[kind]), cols]
        return pltpu.make_async_remote_copy(src_ref=dst, dst_ref=dst, send_sem=d_send.at[kind, k], recv_sem=d_recv.at[kind, k],
                                            device_id={'ep': over if kind == 0 else sib}, device_id_type=MESH)

    for j in range(3):
        for what in range(2):
            idx_copy(j, what).start()
    mine_copy.wait()
    for k in range(n_kb):
        disp_copy(0, k).start()
        disp_copy(1, k).start()

    def start1(i, c):
        for copy in w1_copies(1, i, RING1 + i):
            copy.start()
        return c

    def start2(g, c):
        w2_copy(g, g).start()
        return c

    lax.fori_loop(0, EXTRA, start1, 0)
    lax.fori_loop(0, RING2, start2, 0)

    for j in range(3):
        for what in range(2):
            idx_copy(j, what).wait()

    expert = lax.broadcasted_iota(jnp.int32, (n_exp, tok_dev), 0) + me * n_exp

    def side(ids_ref, gts_ref):
        ids, gts = ids_ref[...], gts_ref[...]
        hit_any = jnp.zeros((n_exp, tok_dev), jnp.int32)
        gate = jnp.zeros((n_exp, tok_dev), F32)
        for j in range(ids.shape[0]):
            hit = ids[j:j + 1, :] == expert
            hit_any = hit_any + jnp.where(hit, 1, 0)
            gate = gate + jnp.where(hit, gts[j:j + 1, :], 0.0)
        return hit_any, gate

    parts = [side(ids_in, gts_in)] + [side(ids_all.at[j], gts_all.at[j]) for j in range(3)]

    def of_device(b, i):
        p = [part[i] for part in parts]
        return jnp.where(me == b, p[0], jnp.where(over == b, p[1], jnp.where(diag == b, p[2], p[3])))

    member = jnp.concatenate([of_device(b, 0) for b in range(GROUPS)], axis=1)
    gate = jnp.concatenate([of_device(b, 1) for b in range(GROUPS)], axis=1)
    lane = lax.broadcasted_iota(jnp.int32, (n_exp, n_tok), 1)
    count = member
    shift = 1
    while shift < n_tok:
        count = count + jnp.where(lane >= shift, pltpu.roll(count, shift, 1), 0)
        shift *= 2
    is_mem = member > 0
    slot = jnp.where(is_mem, count - 1, -1)
    slots[...] = slot
    pos = lax.broadcasted_iota(jnp.int32, (n_exp, n_tok), 0) * CAP + slot
    big = n_exp * CAP
    pos1 = jnp.min(jnp.where(is_mem, pos, big), axis=0, keepdims=True)
    pos2 = jnp.max(jnp.where(is_mem, pos, -1), axis=0, keepdims=True)
    g1 = jnp.sum(jnp.where(is_mem & (pos == pos1), gate, 0.0), axis=0, keepdims=True)
    g2 = jnp.sum(jnp.where(is_mem & (pos == pos2), gate, 0.0), axis=0, keepdims=True)
    sub = lax.broadcasted_iota(jnp.int32, (8, n_tok), 0)
    packed = jnp.where(sub == 0, pos1.astype(F32), jnp.where(sub == 1, pos2.astype(F32), jnp.where(sub == 2, g1, jnp.where(sub == 3, g2, 0.0))))
    tbl[...] = jnp.transpose(packed)

    def clear(i, c):
        acc[pl.ds(pl.multiple_of(i * CAP, CAP), CAP), :] = jnp.zeros((CAP, 2 * ffn), F32)
        return c

    lax.fori_loop(0, n_exp, clear, 0)

    half = big // 2
    pick_rows = n_tok // (n_two * (n_kb - 3))

    def build_picks(i):
        per = tok_dev // pick_rows
        dev, r = lax.div(i, per), pl.multiple_of(lax.rem(i, per) * pick_rows, pick_rows)
        t = tbl[pl.ds(pl.multiple_of(i * pick_rows, pick_rows), pick_rows), :]
        for h in range(2):
            at = (lax.broadcasted_iota(jnp.int32, (pick_rows, half), 1) + h * half).astype(F32)
            for p in range(2):
                ring1[RING1 + dev, h, p, pl.ds(r, pick_rows), :] = jnp.where(t[:, p:p + 1] == at, 1.0, 0.0).astype(BF16)

    def fan(cols, e, n, par):
        at = lax.broadcasted_iota(jnp.int32, (CAP, n_tok), 0)
        hot = jnp.concatenate([jnp.where(at == slots[pl.ds(e + m, 1), :], 1.0, 0.0).astype(BF16) for m in range(n)], axis=0)
        x = jnp.dot(hot, rows_all[:, cols], preferred_element_type=F32).astype(BF16)
        for u in range(2):
            xbuf[par, u] = x[:, u * KU:(u + 1) * KU] if n == 2 else x[u * 2 * CAP:(u + 1) * 2 * CAP, :]

    def down(e, ring, i):
        r = pl.ds(pl.multiple_of(e * CAP, CAP), CAP)
        y_blk[r, :] = jnp.dot(hid[r, :], ring2[ring, i], preferred_element_type=F32).astype(BF16)

    def ffn_in(e, n, rings, par, final, cw):
        for m in range(n):
            ring = rings[m // (n // PER_BODY)]
            r = pl.ds(pl.multiple_of((e + m) * CAP, CAP), CAP)
            for c0 in range(0, ffn, cw):
                acts = []
                for p in range(2):
                    cols = pl.ds(c0, cw)
                    if n == 2:
                        xr = pl.ds(m * CAP, CAP)
                        act = (jnp.dot(xbuf[par, 0, xr, :], ring1[ring, p, 0, :, cols], preferred_element_type=F32) +
                               jnp.dot(xbuf[par, 1, xr, :], ring1[ring, p, 1, :, cols], preferred_element_type=F32))
                    else:
                        act = jnp.dot(xbuf[par, m // 2, pl.ds((m % 2) * CAP, CAP), :], ring1[ring, p, m % 2, :, cols], preferred_element_type=F32)
                    acc_cols = pl.ds(p * ffn + c0, cw)
                    act = acc[r, acc_cols] + act
                    if not final:
                        acc[r, acc_cols] = act
                    acts.append(act)
                if final:
                    hid[r, cols] = (jax.nn.silu(acts[0]) * acts[1]).astype(BF16)

    def take(k):
        disp_arrival(1, k).wait_recv()
        disp_arrival(2, k).wait_recv()

    def hand_on(k):
        disp_arrival(0, k).wait_recv()
        disp_copy(2, k).start()

    def begin(i, slot0, n_slots, k):
        rings = [lax.rem(i * PER_BODY + m + slot0, n_slots) for m in range(PER_BODY)]
        for m in range(PER_BODY):
            for copy in w1_copies(k, 0, rings[m]):
                copy.wait()
        return rings

    def refill(k, i, slot):
        for copy in w1_copies(k, i, slot):
            copy.start()

    hand_on(0)
    take(0)
    fan(block_cols(0), 0, 4, 0)

    def loop_one(i, c):
        @pl.when(i == n_one - 1)
        def _():
            take(1)

        rings = begin(i, 0, RING1 + EXTRA, 0)
        par = lax.rem(i, 2)
        ffn_in(lax.rem(i, n_one) * 4, 4, rings, par, False, ffn)
        nxt = lax.rem(i + 1, 2 * n_one)
        fan(pl.ds(pl.multiple_of(lax.div(nxt, n_one) * KU, KU), KU), lax.rem(nxt, n_one) * 4, 4, 1 - par)

        @pl.when(i < 2)
        def _():
            for m in range(PER_BODY):
                refill(1, i * 2 + m + EXTRA, rings[m])

        @pl.when(i * (i - 4) * (i - 5) * (i - 1) > 0)
        def _():
            for m in range(PER_BODY):
                refill(2, i * 2 + m - 4 - 4 * lax.div(i, 6), rings[m])

        @pl.when(i == n_one - 3)
        def _():
            hand_on(1)

        @pl.when(i == 2 * n_one - 3)
        def _():
            hand_on(2)
        return c

    lax.fori_loop(0, 2 * n_one, loop_one, 0)
    take(2)
    fan(block_cols(2), 0, 2, 0)

    def loop_two(i, c):
        k = 2 + lax.div(i, n_two)

        @pl.when(lax.rem(i, n_two) == n_two - 1)
        def _():
            take(k + 1)

        rings = begin(i, RING1 - EXTRA, RING1, 2)
        par = lax.rem(i, 2)
        ffn_in(lax.rem(i, n_two) * 2, 2, rings, par, False, ffn)
        nxt = i + 1
        fan(block_cols(2 + lax.div(nxt, n_two)), lax.rem(nxt, n_two) * 2, 2, 1 - par)
        build_picks(i)
        for m in range(PER_BODY):
            ahead = i * 2 + m + RING1
            refill(2 + lax.div(ahead, n_exp), lax.rem(ahead, n_exp), rings[m])

        @pl.when(lax.rem(i, n_two) == n_two - 3)
        def _():
            hand_on(k + 1)
        return c

    lax.fori_loop(0, n_two * (n_kb - 3), loop_two, 0)
    for g in range(RING2):
        w2_copy(g, g).wait()

    def loop_last(i, c):
        rings = begin(i, RING1 - EXTRA, RING1, 2)
        par = lax.rem(i, 2)
        ffn_in(i * 2, 2, rings, par, True, DB)
        fan(block_cols(n_kb - 1), lax.rem(i + 1, n_two) * 2, 2, 1 - par)
        before = lax.rem(i + n_two - 1, n_two) * 2
        for m in range(2):
            down(before + m, lax.div(before, EPS), lax.rem(before, EPS) + m)

        @pl.when(i * 2 + RING1 < n_exp)
        def _():
            for m in range(PER_BODY):
                refill(n_kb - 1, i * 2 + m + RING1, rings[m])
        return c

    lax.fori_loop(0, n_two, loop_last, 0)
    for m in range(2):
        down(n_exp - 2 + m, n_grp - 1, EPS - 2 + m)

    def refill2(g, c):
        w2_copy(n_grp + g, g).start()
        return c

    lax.fori_loop(0, RING2, refill2, 0)

    for k in range(n_kb):
        for kind in range(3):
            disp_copy(kind, k).wait_send()

    def stage(slot, d):
        per = ffn // DB
        return (slot, 0, lax.div(d, per), slice(None), pl.ds(pl.multiple_of(lax.rem(d, per) * DB, DB), DB))

    def ret_copy(j, d):
        cols = pl.ds(pl.multiple_of(d * DB, DB), DB)
        return pltpu.make_async_remote_copy(src_ref=rows_all.at[rows_of(peers[j]), cols], dst_ref=back.at[j, :, cols],
                                            send_sem=r_send.at[j, d], recv_sem=r_recv.at[j, d], device_id={'ep': peers[j]}, device_id_type=MESH)

    def combine(d):
        cols = pl.ds(pl.multiple_of(d * DB, DB), DB)

        def one(j, c):
            dev = lax.rem(me + (sib - me) * lax.rem(lax.div(j + 1, 2), 2) + 2 - 2 * lax.div(j, 2), GROUPS)
            r = rows_of(dev)
            y1, y2 = (sum(jnp.dot(ring1[RING1 + dev, h, p], y_blk[h * half:(h + 1) * half, :], preferred_element_type=F32) for h in range(2)) for p in range(2))
            sums = (tbl[r, 2:3] * y1 + tbl[r, 3:4] * y2).astype(BF16)

            @pl.when(j < 3)
            def _():
                rows_all[r, cols] = sums
                pltpu.make_async_remote_copy(src_ref=rows_all.at[r, cols], dst_ref=back.at[j, :, cols], send_sem=r_send.at[j, d], recv_sem=r_recv.at[j, d],
                                             device_id={'ep': dev}, device_id_type=MESH).start()

            @pl.when(j == 3)
            def _():
                ring1[stage(0, d)] = sums
            return c

        lax.fori_loop(0, GROUPS, one, 0)

    def block2(d, c):
        def step2(g, c2):
            step = d * n_grp + g
            ring = lax.rem(step, RING2)
            w2_copy(step, ring).wait()
            for i in range(EPS):
                down(g * EPS + i, ring, i)

            @pl.when(step + RING2 < steps2)
            def _():
                w2_copy(step + RING2, ring).start()
            return c2

        @pl.when(d > 0)
        def _():
            lax.fori_loop(0, n_grp, step2, 0)

        combine(d)
        return c

    lax.fori_loop(0, n_db, block2, 0)

    def out_copy(d):
        cols = pl.ds(pl.multiple_of(d * DB, DB), DB)
        return pltpu.make_async_copy(ring1.at[stage(1, d)], out.at[:, cols], o_sem.at[d])

    def finish(d, c):
        cols = pl.ds(pl.multiple_of(d * DB, DB), DB)
        for j in range(3):
            ret_copy(j, d).wait_recv()
        total = rows_all[rows_of(me), cols].astype(F32) + ring1[stage(0, d)].astype(F32)
        for j in range(3):
            total = total + back[j, :, cols].astype(F32)
        ring1[stage(1, d)] = total.astype(BF16)
        out_copy(d).start()
        return c

    lax.fori_loop(0, n_db, finish, 0)

    def drain(d, c):
        for j in range(3):
            ret_copy(j, d).wait_send()
        out_copy(d).wait()
        return c

    lax.fori_loop(0, n_db, drain, 0)


def solution(mesh):
    row_spec = P(('dp', 'ep'))
    expert_spec = P('ep')

    def device_step(tokens, expert_ids, gate_vals, w_gate, w_up, w_down):
        tok_dev, d_model = tokens.shape
        n_exp, _, ffn = w_gate.shape
        top_k = expert_ids.shape[1]
        n_tok = GROUPS * tok_dev
        pairs = n_exp * CAP
        units = (n_exp, d_model // KU, KU, ffn)
        hbm = pl.BlockSpec(memory_space=pltpu.HBM)
        vmem = pl.BlockSpec(memory_space=pltpu.VMEM)
        dma = pltpu.SemaphoreType.DMA
        return pl.pallas_call(
            layer_kernel,
            out_shape=jax.ShapeDtypeStruct((tok_dev, d_model), BF16),
            in_specs=[hbm, vmem, vmem, hbm, hbm, hbm],
            out_specs=hbm,
            scratch_shapes=[
                pltpu.VMEM((pairs, 2 * ffn), F32),
                pltpu.VMEM((n_tok, d_model), BF16),
                pltpu.VMEM((pairs, ffn), BF16),
                pltpu.VMEM((RING1 + EXTRA, 2, 2, KU, ffn), BF16),
                pltpu.VMEM((RING2, EPS, ffn, DB), BF16),
                pltpu.VMEM((3, tok_dev, d_model), BF16),
                pltpu.VMEM((pairs, DB), BF16),
                pltpu.VMEM((2, 2, 2 * CAP, KU), BF16),
                pltpu.VMEM((3, top_k, tok_dev), jnp.int32),
                pltpu.VMEM((3, top_k, tok_dev), F32),
                pltpu.VMEM((n_exp, n_tok), jnp.int32),
                pltpu.VMEM((n_tok, 8), F32),
                dma((RING1 + EXTRA, 2)),
                dma((RING2,)),
                dma((1,)),
                dma((2, 3)),
                dma((2, 3)),
                dma((3, 2 + (d_model // KU - 2) // 2)),
                dma((3, 2 + (d_model // KU - 2) // 2)),
                dma((3, d_model // DB)),
                dma((3, d_model // DB)),
                dma((d_model // DB,)),
            ],
            compiler_params=pltpu.CompilerParams(collective_id=0, has_side_effects=True, vmem_limit_bytes=67043328),
        )(tokens, expert_ids.T, gate_vals.T, w_gate.reshape(units), w_up.reshape(units), w_down)

    return jax.shard_map(device_step, mesh=mesh, in_specs=(row_spec, row_spec, row_spec, expert_spec, expert_spec, expert_spec), out_specs=row_spec, check_vma=False)
```

time: 107 us -> 101 us (0.944)
  Pallas kernels: 105 us -> 98.3 us
    pallas_call x1, Pallas kernels: 105 us -> 98.3 us  [device_step(): pl.pallas_call(layer_kernel, out_shape=jax.ShapeDtypeStruct((tok_dev, d_m...]
where the time goes in v4:
time: 101 us
  Pallas kernels  98.3 us (97%)
  local copies, waits for them, and re-layouts  2.3 us (2%)
    pallas_call x1, Pallas kernels, device_step(): pl.pallas_call(layer_kernel, out_shape=jax.ShapeDtypeStruct((tok_dev, d_m...  98.3 us
    unnamed x1, local copies, waits for them, and re-layouts  2.3 us

profile of v4, /device:TPU:0, one launch (start us, length us, event | category | flops | bytes accessed | tf_op | source)
XLA Modules:
  0.0 100.6 jit_solution(15208206215376679633)
XLA Ops:
  0.0 98.3 %shard_map.64 = bf16[256,2048]{1,0:T(8,128)(2,1)} custom-call(bf16[256,2048]{1,0:T(8,128)(2,1)} %tok.1, s32[8,256]{1,0:T(8,128)} %bitcast.4, f32[8,256]{1,0:T(8,128)} %bitcast.5, bf16[16,8,256,1024]{3,2,1,0:T(8,128)(2,1)} %bitcast.2.w_gate, bf16[16,8,256,1024]{3,2,1,0:T(8,128)(2,1)} %bitcast.3.w_up, bf16[16,1024,2048]{2,1,0:T(8,128)(2,1)} %w_down.1), custom_call_target="tpu_custom_call" | custom-call | tf_op jit(solution)/shard_map/pallas_call | solution.py:411
  98.3 2.3 %copy.8 = bf16[256,2048]{1,0:T(8,128)(2,1)} copy(bf16[256,2048]{1,0:T(8,128)(2,1)} %shard_map.64) | data formatting | bytes 2097152

commit v5 on v4

--- a/solution.py
+++ b/solution.py
@@ -1,3 +1,5 @@
+import functools
+
 import jax
 import jax.numpy as jnp
 from jax import lax
@@ -16,16 +18,18 @@
 PER_BODY = 2
 EPS = 4
 RING2 = 4
-
-
-def layer_kernel(tok, ids_in, gts_in, w_gate, w_up, w_down, out, acc, rows_all, hid, ring1, ring2, back,
-                 y_blk, xbuf, ids_all, gts_all, slots, tbl, w1_sem, w2_sem, loc_sem, idx_send, idx_recv, d_send, d_recv,
+FINAL_COLS = 512
+
+
+def layer_kernel(tok, ids_hbm, gts_hbm, w_gate, w_up, w_down, out, acc, rows_all, hid, ring1, ring2, back,
+                 y_blk, xbuf, ids_in, gts_in, ids_all, gts_all, slots, tbl, w1_sem, w2_sem, loc_sem, idx_send, idx_recv, d_send, d_recv,
                  r_send, r_recv, o_sem):
     tok_dev, d_model = tok.shape
     n_exp, n_unit, _, ffn = w_gate.shape
     n_tok = GROUPS * tok_dev
     n_kb, n_db, n_grp = 2 + (n_unit - 2) // 2, d_model // DB, n_exp // EPS
-    n_one, n_two = n_exp // 4, n_exp // 2
+    n_one, n_two = n_exp // (2 * PER_BODY), n_exp // PER_BODY
+    assert EPS % PER_BODY == 0 and n_exp == GROUPS * EPS and n_one * PER_BODY == RING1 == 2 * EXTRA
     steps2 = n_db * n_grp
 
     me = lax.axis_index('ep')
@@ -40,13 +44,16 @@
     def first_unit(k):
         return k if isinstance(k, int) and k < 2 else 2 * k - 2
 
+    def pair_of(slot):
+        return lax.div(slot, 2)
+
     def w1_copies(k, i, slot):
         if isinstance(k, int) and k < 2:
             part = (pl.ds(i * 2, 2), k)
         else:
             part = (i, pl.ds(first_unit(k), 2))
-        return (pltpu.make_async_copy(w_gate.at[part], ring1.at[slot, 0], w1_sem.at[slot, 0]),
-                pltpu.make_async_copy(w_up.at[part], ring1.at[slot, 1], w1_sem.at[slot, 1]))
+        return (pltpu.make_async_copy(w_gate.at[part], ring1.at[slot, 0], w1_sem.at[pair_of(slot)]),
+                pltpu.make_async_copy(w_up.at[part], ring1.at[slot, 1], w1_sem.at[pair_of(slot)]))
 
     def block_cols(k):
         if isinstance(k, int):
@@ -60,6 +67,10 @@
 
     mine_copy = pltpu.make_async_copy(tok, rows_all.at[rows_of(me), :], loc_sem.at[0])
     mine_copy.start()
+    ids_copy = pltpu.make_async_copy(ids_hbm, ids_in, loc_sem.at[1])
+    gts_copy = pltpu.make_async_copy(gts_hbm, gts_in, loc_sem.at[2])
+    ids_copy.start()
+    gts_copy.start()
     barrier = pltpu.get_barrier_semaphore()
     for dev in peers:
         pl.semaphore_signal(barrier, inc=1, device_id={'ep': dev}, device_id_type=MESH)
@@ -89,11 +100,15 @@
         return pltpu.make_async_remote_copy(src_ref=dst, dst_ref=dst, send_sem=d_send.at[kind, k], recv_sem=d_recv.at[kind, k],
                                             device_id={'ep': over if kind == 0 else sib}, device_id_type=MESH)
 
+    mine_copy.wait()
+    disp_copy(0, 0).start()
+    disp_copy(1, 0).start()
+    ids_copy.wait()
+    gts_copy.wait()
     for j in range(3):
         for what in range(2):
             idx_copy(j, what).start()
-    mine_copy.wait()
-    for k in range(n_kb):
+    for k in range(1, n_kb):
         disp_copy(0, k).start()
         disp_copy(1, k).start()
 
@@ -150,53 +165,47 @@
     g2 = jnp.sum(jnp.where(is_mem & (pos == pos2), gate, 0.0), axis=0, keepdims=True)
     sub = lax.broadcasted_iota(jnp.int32, (8, n_tok), 0)
     packed = jnp.where(sub == 0, pos1.astype(F32), jnp.where(sub == 1, pos2.astype(F32), jnp.where(sub == 2, g1, jnp.where(sub == 3, g2, 0.0))))
-    tbl[...] = jnp.transpose(packed)
-
-    def clear(i, c):
-        acc[pl.ds(pl.multiple_of(i * CAP, CAP), CAP), :] = jnp.zeros((CAP, 2 * ffn), F32)
-        return c
-
-    lax.fori_loop(0, n_exp, clear, 0)
+    tbl[...] = packed
 
     half = big // 2
-    pick_rows = n_tok // (n_two * (n_kb - 3))
 
     def build_picks(i):
-        per = tok_dev // pick_rows
-        dev, r = lax.div(i, per), pl.multiple_of(lax.rem(i, per) * pick_rows, pick_rows)
-        t = tbl[pl.ds(pl.multiple_of(i * pick_rows, pick_rows), pick_rows), :]
-        for h in range(2):
-            at = (lax.broadcasted_iota(jnp.int32, (pick_rows, half), 1) + h * half).astype(F32)
-            for p in range(2):
-                ring1[RING1 + dev, h, p, pl.ds(r, pick_rows), :] = jnp.where(t[:, p:p + 1] == at, 1.0, 0.0).astype(BF16)
+        b, h = (i // 2, i % 2) if isinstance(i, int) else (lax.div(i, 2), lax.rem(i, 2))
+        per = tok_dev // CAP
+        dev, r = (b // per, b % per * CAP) if isinstance(i, int) else (lax.div(b, per), pl.multiple_of(lax.rem(b, per) * CAP, CAP))
+        t = jnp.transpose(tbl[:, pl.ds(b * CAP if isinstance(i, int) else pl.multiple_of(b * CAP, CAP), CAP)])
+        at = (lax.broadcasted_iota(jnp.int32, (CAP, half), 1) + h * half).astype(F32)
+        for p in range(2):
+            ring1[RING1 + dev, h, p, pl.ds(r, CAP), :] = jnp.where(t[:, p:p + 1] == at, 1.0, 0.0).astype(BF16)
 
     def fan(cols, e, n, par):
         at = lax.broadcasted_iota(jnp.int32, (CAP, n_tok), 0)
-        hot = jnp.concatenate([jnp.where(at == slots[pl.ds(e + m, 1), :], 1.0, 0.0).astype(BF16) for m in range(n)], axis=0)
-        x = jnp.dot(hot, rows_all[:, cols], preferred_element_type=F32).astype(BF16)
-        for u in range(2):
-            xbuf[par, u] = x[:, u * KU:(u + 1) * KU] if n == 2 else x[u * 2 * CAP:(u + 1) * 2 * CAP, :]
+        for q in range(n // 2):
+            hot = jnp.concatenate([jnp.where(at == slots[pl.ds(e + 2 * q + m, 1), :], 1.0, 0.0).astype(BF16) for m in range(2)], axis=0)
+            x = jnp.dot(hot, rows_all[:, cols], preferred_element_type=F32).astype(BF16)
+            for u in range(x.shape[1] // KU):
+                xbuf[par, u, q] = x[:, u * KU:(u + 1) * KU]
 
     def down(e, ring, i):
         r = pl.ds(pl.multiple_of(e * CAP, CAP), CAP)
         y_blk[r, :] = jnp.dot(hid[r, :], ring2[ring, i], preferred_element_type=F32).astype(BF16)
 
-    def ffn_in(e, n, rings, par, final, cw):
-        for m in range(n):
-            ring = rings[m // (n // PER_BODY)]
+    def ffn_in(e, rings, par, two, first, final, cw):
+        for m in range(len(rings) * (1 if two else 2)):
+            ring, xr = rings[m if two else m // 2], pl.ds((m % 2) * CAP, CAP)
             r = pl.ds(pl.multiple_of((e + m) * CAP, CAP), CAP)
             for c0 in range(0, ffn, cw):
                 acts = []
                 for p in range(2):
                     cols = pl.ds(c0, cw)
-                    if n == 2:
-                        xr = pl.ds(m * CAP, CAP)
-                        act = (jnp.dot(xbuf[par, 0, xr, :], ring1[ring, p, 0, :, cols], preferred_element_type=F32) +
-                               jnp.dot(xbuf[par, 1, xr, :], ring1[ring, p, 1, :, cols], preferred_element_type=F32))
+                    if two:
+                        act = (jnp.dot(xbuf[par, 0, m // 2, xr, :], ring1[ring, p, 0, :, cols], preferred_element_type=F32) +
+                               jnp.dot(xbuf[par, 1, m // 2, xr, :], ring1[ring, p, 1, :, cols], preferred_element_type=F32))
                     else:
-                        act = jnp.dot(xbuf[par, m // 2, pl.ds((m % 2) * CAP, CAP), :], ring1[ring, p, m % 2, :, cols], preferred_element_type=F32)
+                        act = jnp.dot(xbuf[par, 0, m // 2, xr, :], ring1[ring, p, m % 2, :, cols], preferred_element_type=F32)
                     acc_cols = pl.ds(p * ffn + c0, cw)
-                    act = acc[r, acc_cols] + act
+                    if not first:
+                        act = acc[r, acc_cols] + act
                     if not final:
                         acc[r, acc_cols] = act
                     acts.append(act)
@@ -211,99 +220,73 @@
         disp_arrival(0, k).wait_recv()
         disp_copy(2, k).start()
 
-    def begin(i, slot0, n_slots, k):
-        rings = [lax.rem(i * PER_BODY + m + slot0, n_slots) for m in range(PER_BODY)]
-        for m in range(PER_BODY):
-            for copy in w1_copies(k, 0, rings[m]):
-                copy.wait()
-        return rings
+    def begin(k, i):
+        rem = (lambda a, b: a % b) if isinstance(i, int) else lax.rem
+        slot = i * PER_BODY if k == 0 else rem(i * PER_BODY + RING1, RING1 + EXTRA) if k == 1 else rem(i * PER_BODY + RING1 - EXTRA, RING1)
+        both = ring1.at[pl.ds(slot, PER_BODY)]
+        pltpu.make_async_copy(both, both, w1_sem.at[pair_of(slot)]).wait()
+        return [slot + m for m in range(PER_BODY)]
 
     def refill(k, i, slot):
         for copy in w1_copies(k, i, slot):
             copy.start()
 
+    def body(k, i, nxt, before=None):
+        static = isinstance(i, int)
+        two, final = k >= 2, k == n_kb - 1
+        per, n_body = (PER_BODY, n_two) if two else (2 * PER_BODY, n_one)
+        par = i % 2 if static else lax.rem(i, 2)
+        rings = begin(k, i)
+        ffn_in(i * per, rings, par, two, k == 0, final, FINAL_COLS if final else ffn)
+        if nxt is not None:
+            fan(block_cols(nxt[0]), nxt[1] * (PER_BODY if nxt[0] >= 2 else 2 * PER_BODY), PER_BODY if nxt[0] >= 2 else 2 * PER_BODY, 1 - par)
+        if before is not None:
+            for m in range(PER_BODY):
+                e = before * PER_BODY + m
+                down(e, lax.div(e, EPS), lax.rem(e, EPS))
+        if 2 <= k < 4:
+            build_picks((k - 2) * n_body + i)
+
+        def fill(kk, i0):
+            for m in range(PER_BODY):
+                refill(kk, i0 + m, rings[m])
+
+        here, s0 = n_body * PER_BODY, i * PER_BODY
+        when = (lambda c: (lambda f: f() if c else None)) if static else pl.when
+        if k == 0:
+            when(i < 2)(lambda: fill(1, s0 + EXTRA))
+            when(i >= 2)(lambda: fill(2, s0 - EXTRA))
+        elif k == 1:
+            when(i >= 2)(lambda: fill(2, s0))
+        elif final:
+            when(s0 + RING1 < here)(lambda: fill(k, s0 + RING1))
+        elif static:
+            fill(k + (s0 + RING1) // here, (s0 + RING1) % here)
+        else:
+            fill(k + lax.div(s0 + RING1, here), lax.rem(s0 + RING1, here))
+
     hand_on(0)
     take(0)
-    fan(block_cols(0), 0, 4, 0)
-
-    def loop_one(i, c):
-        @pl.when(i == n_one - 1)
-        def _():
-            take(1)
-
-        rings = begin(i, 0, RING1 + EXTRA, 0)
-        par = lax.rem(i, 2)
-        ffn_in(lax.rem(i, n_one) * 4, 4, rings, par, False, ffn)
-        nxt = lax.rem(i + 1, 2 * n_one)
-        fan(pl.ds(pl.multiple_of(lax.div(nxt, n_one) * KU, KU), KU), lax.rem(nxt, n_one) * 4, 4, 1 - par)
-
-        @pl.when(i < 2)
-        def _():
-            for m in range(PER_BODY):
-                refill(1, i * 2 + m + EXTRA, rings[m])
-
-        @pl.when(i * (i - 4) * (i - 5) * (i - 1) > 0)
-        def _():
-            for m in range(PER_BODY):
-                refill(2, i * 2 + m - 4 - 4 * lax.div(i, 6), rings[m])
-
-        @pl.when(i == n_one - 3)
-        def _():
-            hand_on(1)
-
-        @pl.when(i == 2 * n_one - 3)
-        def _():
-            hand_on(2)
-        return c
-
-    lax.fori_loop(0, 2 * n_one, loop_one, 0)
-    take(2)
-    fan(block_cols(2), 0, 2, 0)
-
-    def loop_two(i, c):
-        k = 2 + lax.div(i, n_two)
-
-        @pl.when(lax.rem(i, n_two) == n_two - 1)
-        def _():
+    fan(block_cols(0), 0, 2 * PER_BODY, 0)
+    for k in range(n_kb):
+        n_body, final = n_two if k >= 2 else n_one, k == n_kb - 1
+        if final:
+            for g in range(RING2):
+                w2_copy(g, g).wait()
+
+        def loop(i, c, k=k, n_body=n_body, final=final):
+            body(k, i, (k, i + 1), lax.rem(i + n_body - 1, n_body) if final else None)
+            if not final:
+                pl.when(i == n_body - 3)(functools.partial(hand_on, k + 1))
+            return c
+
+        lax.fori_loop(0, n_body - 1, loop, 0)
+        if not final:
             take(k + 1)
-
-        rings = begin(i, RING1 - EXTRA, RING1, 2)
-        par = lax.rem(i, 2)
-        ffn_in(lax.rem(i, n_two) * 2, 2, rings, par, False, ffn)
-        nxt = i + 1
-        fan(block_cols(2 + lax.div(nxt, n_two)), lax.rem(nxt, n_two) * 2, 2, 1 - par)
-        build_picks(i)
-        for m in range(PER_BODY):
-            ahead = i * 2 + m + RING1
-            refill(2 + lax.div(ahead, n_exp), lax.rem(ahead, n_exp), rings[m])
-
-        @pl.when(lax.rem(i, n_two) == n_two - 3)
-        def _():
-            hand_on(k + 1)
-        return c
-
-    lax.fori_loop(0, n_two * (n_kb - 3), loop_two, 0)
-    for g in range(RING2):
-        w2_copy(g, g).wait()
-
-    def loop_last(i, c):
-        rings = begin(i, RING1 - EXTRA, RING1, 2)
-        par = lax.rem(i, 2)
-        ffn_in(i * 2, 2, rings, par, True, DB)
-        fan(block_cols(n_kb - 1), lax.rem(i + 1, n_two) * 2, 2, 1 - par)
-        before = lax.rem(i + n_two - 1, n_two) * 2
-        for m in range(2):
-            down(before + m, lax.div(before, EPS), lax.rem(before, EPS) + m)
-
-        @pl.when(i * 2 + RING1 < n_exp)
-        def _():
-            for m in range(PER_BODY):
-                refill(n_kb - 1, i * 2 + m + RING1, rings[m])
-        return c
-
-    lax.fori_loop(0, n_two, loop_last, 0)
-    for m in range(2):
-        down(n_exp - 2 + m, n_grp - 1, EPS - 2 + m)
+        body(k, n_body - 1, None if final else (k + 1, 0), n_body - 2 if final else None)
+
+    for m in range(EPS - PER_BODY, EPS):
+        down(n_exp - EPS + m, n_grp - 1, m)
 
     def refill2(g, c):
         w2_copy(n_grp + g, g).start()
@@ -331,7 +314,8 @@
             dev = lax.rem(me + (sib - me) * lax.rem(lax.div(j + 1, 2), 2) + 2 - 2 * lax.div(j, 2), GROUPS)
             r = rows_of(dev)
             y1, y2 = (sum(jnp.dot(ring1[RING1 + dev, h, p], y_blk[h * half:(h + 1) * half, :], preferred_element_type=F32) for h in range(2)) for p in range(2))
-            sums = (tbl[r, 2:3] * y1 + tbl[r, 3:4] * y2).astype(BF16)
+            t = jnp.transpose(tbl[:, r])
+            sums = (t[:, 2:3] * y1 + t[:, 3:4] * y2).astype(BF16)
 
             @pl.when(j < 3)
             def _():
@@ -406,12 +390,11 @@
         pairs = n_exp * CAP
         units = (n_exp, d_model // KU, KU, ffn)
         hbm = pl.BlockSpec(memory_space=pltpu.HBM)
-        vmem = pl.BlockSpec(memory_space=pltpu.VMEM)
         dma = pltpu.SemaphoreType.DMA
         return pl.pallas_call(
             layer_kernel,
             out_shape=jax.ShapeDtypeStruct((tok_dev, d_model), BF16),
-            in_specs=[hbm, vmem, vmem, hbm, hbm, hbm],
+            in_specs=[hbm] * 6,
             out_specs=hbm,
             scratch_shapes=[
                 pltpu.VMEM((pairs, 2 * ffn), F32),
@@ -421,14 +404,16 @@
                 pltpu.VMEM((RING2, EPS, ffn, DB), BF16),
                 pltpu.VMEM((3, tok_dev, d_model), BF16),
                 pltpu.VMEM((pairs, DB), BF16),
-                pltpu.VMEM((2, 2, 2 * CAP, KU), BF16),
+                pltpu.VMEM((2, 2, 2, 2 * CAP, KU), BF16),
+                pltpu.VMEM((top_k, tok_dev), jnp.int32),
+                pltpu.VMEM((top_k, tok_dev), F32),
                 pltpu.VMEM((3, top_k, tok_dev), jnp.int32),
                 pltpu.VMEM((3, top_k, tok_dev), F32),
                 pltpu.VMEM((n_exp, n_tok), jnp.int32),
-                pltpu.VMEM((n_tok, 8), F32),
-                dma((RING1 + EXTRA, 2)),
+                pltpu.VMEM((8, n_tok), F32),
+                dma(((RING1 + EXTRA) // 2,)),
                 dma((RING2,)),
-                dma((1,)),
+                dma((3,)),
                 dma((2, 3)),
                 dma((2, 3)),
                 dma((3, 2 + (d_model // KU - 2) // 2)),

time: 101 us -> 99.2 us (0.982)
  Pallas kernels: 98.3 us -> 96.8 us
    pallas_call x1, Pallas kernels: 98.3 us -> 96.8 us  [device_step(): pl.pallas_call(layer_kernel, out_shape=jax.ShapeDtypeStruct((tok_dev, d_m...]
where the time goes in v5:
time: 99.2 us; the launch traced here: 99.1 us
  Pallas kernels  96.8 us (98%)
  local copies, waits for them, and re-layouts  2.3 us (2%)
    pallas_call x1, Pallas kernels, device_step(): pl.pallas_call(layer_kernel, out_shape=jax.ShapeDtypeStruct((tok_dev, d_m...  96.8 us
    unnamed x1, local copies, waits for them, and re-layouts  2.3 us

profile of v5, /device:TPU:0, one launch (start us, length us, event | category | flops | bytes accessed | tf_op | source)
XLA Modules:
  0.0 99.1 jit_solution(8327016134101498148)
XLA Ops:
  0.0 96.8 %shard_map.64 = bf16[256,2048]{1,0:T(8,128)(2,1)} custom-call(bf16[256,2048]{1,0:T(8,128)(2,1)} %tok.1, s32[8,256]{1,0:T(8,128)} %bitcast.4, f32[8,256]{1,0:T(8,128)} %bitcast.5, bf16[16,8,256,1024]{3,2,1,0:T(8,128)(2,1)} %bitcast.2.w_gate, bf16[16,8,256,1024]{3,2,1,0:T(8,128)(2,1)} %bitcast.3.w_up, bf16[16,1024,2048]{2,1,0:T(8,128)(2,1)} %w_down.1), custom_call_target="tpu_custom_call" | custom-call | tf_op jit(solution)/shard_map/pallas_call | solution.py:394
  96.8 2.3 %copy.8 = bf16[256,2048]{1,0:T(8,128)(2,1)} copy(bf16[256,2048]{1,0:T(8,128)(2,1)} %shard_map.64) | data formatting | bytes 2097152

commit v6 on v5

--- a/solution.py
+++ b/solution.py
@@ -23,7 +23,7 @@
 
 def layer_kernel(tok, ids_hbm, gts_hbm, w_gate, w_up, w_down, out, acc, rows_all, hid, ring1, ring2, back,
                  y_blk, xbuf, ids_in, gts_in, ids_all, gts_all, slots, tbl, w1_sem, w2_sem, loc_sem, idx_send, idx_recv, d_send, d_recv,
-                 r_send, r_recv, o_sem):
+                 r_send, r_recv):
     tok_dev, d_model = tok.shape
     n_exp, n_unit, _, ffn = w_gate.shape
     n_tok = GROUPS * tok_dev
@@ -66,11 +66,11 @@
         return pltpu.make_async_copy(w_down.at[pl.ds(g * EPS, EPS), :, cols], ring2.at[slot], w2_sem.at[slot])
 
     mine_copy = pltpu.make_async_copy(tok, rows_all.at[rows_of(me), :], loc_sem.at[0])
-    mine_copy.start()
     ids_copy = pltpu.make_async_copy(ids_hbm, ids_in, loc_sem.at[1])
     gts_copy = pltpu.make_async_copy(gts_hbm, gts_in, loc_sem.at[2])
     ids_copy.start()
     gts_copy.start()
+    mine_copy.start()
     barrier = pltpu.get_barrier_semaphore()
     for dev in peers:
         pl.semaphore_signal(barrier, inc=1, device_id={'ep': dev}, device_id_type=MESH)
@@ -100,15 +100,13 @@
         return pltpu.make_async_remote_copy(src_ref=dst, dst_ref=dst, send_sem=d_send.at[kind, k], recv_sem=d_recv.at[kind, k],
                                             device_id={'ep': over if kind == 0 else sib}, device_id_type=MESH)
 
-    mine_copy.wait()
-    disp_copy(0, 0).start()
-    disp_copy(1, 0).start()
     ids_copy.wait()
     gts_copy.wait()
     for j in range(3):
         for what in range(2):
             idx_copy(j, what).start()
-    for k in range(1, n_kb):
+    mine_copy.wait()
+    for k in range(n_kb):
         disp_copy(0, k).start()
         disp_copy(1, k).start()
 
@@ -184,7 +182,7 @@
             hot = jnp.concatenate([jnp.where(at == slots[pl.ds(e + 2 * q + m, 1), :], 1.0, 0.0).astype(BF16) for m in range(2)], axis=0)
             x = jnp.dot(hot, rows_all[:, cols], preferred_element_type=F32).astype(BF16)
             for u in range(x.shape[1] // KU):
-                xbuf[par, u, q] = x[:, u * KU:(u + 1) * KU]
+                xbuf[par, q + u] = x[:, u * KU:(u + 1) * KU]
 
     def down(e, ring, i):
         r = pl.ds(pl.multiple_of(e * CAP, CAP), CAP)
@@ -199,10 +197,10 @@
                 for p in range(2):
                     cols = pl.ds(c0, cw)
                     if two:
-                        act = (jnp.dot(xbuf[par, 0, m // 2, xr, :], ring1[ring, p, 0, :, cols], preferred_element_type=F32) +
-                               jnp.dot(xbuf[par, 1, m // 2, xr, :], ring1[ring, p, 1, :, cols], preferred_element_type=F32))
+                        act = (jnp.dot(xbuf[par, 0, xr, :], ring1[ring, p, 0, :, cols], preferred_element_type=F32) +
+                               jnp.dot(xbuf[par, 1, xr, :], ring1[ring, p, 1, :, cols], preferred_element_type=F32))
                     else:
-                        act = jnp.dot(xbuf[par, 0, m // 2, xr, :], ring1[ring, p, m % 2, :, cols], preferred_element_type=F32)
+                        act = jnp.dot(xbuf[par, m // 2, xr, :], ring1[ring, p, m % 2, :, cols], preferred_element_type=F32)
                     acc_cols = pl.ds(p * ffn + c0, cw)
                     if not first:
                         act = acc[r, acc_cols] + act
@@ -352,10 +350,6 @@
 
     lax.fori_loop(0, n_db, block2, 0)
 
-    def out_copy(d):
-        cols = pl.ds(pl.multiple_of(d * DB, DB), DB)
-        return pltpu.make_async_copy(ring1.at[stage(1, d)], out.at[:, cols], o_sem.at[d])
-
     def finish(d, c):
         cols = pl.ds(pl.multiple_of(d * DB, DB), DB)
         for j in range(3):
@@ -363,8 +357,7 @@
         total = rows_all[rows_of(me), cols].astype(F32) + ring1[stage(0, d)].astype(F32)
         for j in range(3):
             total = total + back[j, :, cols].astype(F32)
-        ring1[stage(1, d)] = total.astype(BF16)
-        out_copy(d).start()
+        out[:, cols] = total.astype(BF16)
         return c
 
     lax.fori_loop(0, n_db, finish, 0)
@@ -372,7 +365,6 @@
     def drain(d, c):
         for j in range(3):
             ret_copy(j, d).wait_send()
-        out_copy(d).wait()
         return c
 
     lax.fori_loop(0, n_db, drain, 0)
@@ -393,9 +385,9 @@
         dma = pltpu.SemaphoreType.DMA
         return pl.pallas_call(
             layer_kernel,
-            out_shape=jax.ShapeDtypeStruct((tok_dev, d_model), BF16),
+            out_shape=pltpu.VMEM((tok_dev, d_model), BF16),
             in_specs=[hbm] * 6,
-            out_specs=hbm,
+            out_specs=pl.BlockSpec(memory_space=pltpu.VMEM),
             scratch_shapes=[
                 pltpu.VMEM((pairs, 2 * ffn), F32),
                 pltpu.VMEM((n_tok, d_model), BF16),
@@ -404,7 +396,7 @@
                 pltpu.VMEM((RING2, EPS, ffn, DB), BF16),
                 pltpu.VMEM((3, tok_dev, d_model), BF16),
                 pltpu.VMEM((pairs, DB), BF16),
-                pltpu.VMEM((2, 2, 2, 2 * CAP, KU), BF16),
+                pltpu.VMEM((2, 2, 2 * CAP, KU), BF16),
                 pltpu.VMEM((top_k, tok_dev), jnp.int32),
                 pltpu.VMEM((top_k, tok_dev), F32),
                 pltpu.VMEM((3, top_k, tok_dev), jnp.int32),
@@ -420,9 +412,8 @@
                 dma((3, 2 + (d_model // KU - 2) // 2)),
                 dma((3, d_model // DB)),
                 dma((3, d_model // DB)),
-                dma((d_model // DB,)),
             ],
-            compiler_params=pltpu.CompilerParams(collective_id=0, has_side_effects=True, vmem_limit_bytes=67043328),
+            compiler_params=pltpu.CompilerParams(collective_id=0, has_side_effects=True, vmem_limit_bytes=65800000),
         )(tokens, expert_ids.T, gate_vals.T, w_gate.reshape(units), w_up.reshape(units), w_down)
 
     return jax.shard_map(device_step, mesh=mesh, in_specs=(row_spec, row_spec, row_spec, expert_spec, expert_spec, expert_spec), out_specs=row_spec, check_vma=False)

time: 99.2 us -> 97.2 us (0.980)
  local copies, waits for them, and re-layouts: 2.3 us -> 0.97 us
    unnamed x1, local copies, waits for them, and re-layouts: 2.3 us -> 0.97 us
where the time goes in v6:
time: 97.2 us; the launch traced here: 97.1 us
  Pallas kernels  96.1 us (99%)
    pallas_call x1, Pallas kernels, device_step(): pl.pallas_call(layer_kernel, out_shape=pltpu.VMEM((tok_dev, d_model), BF1...  96.1 us

profile of v6, /device:TPU:0, one launch (start us, length us, event | category | flops | bytes accessed | tf_op | source)
XLA Modules:
  0.0 97.1 jit_solution(9149353863536378952)
XLA Ops:
  0.0 96.1 %shard_map.64 = bf16[256,2048]{1,0:T(8,128)(2,1)S(1)} custom-call(bf16[256,2048]{1,0:T(8,128)(2,1)} %tok.1, s32[8,256]{1,0:T(8,128)} %bitcast.4, f32[8,256]{1,0:T(8,128)} %bitcast.5, bf16[16,8,256,1024]{3,2,1,0:T(8,128)(2,1)} %bitcast.2.w_gate, bf16[16,8,256,1024]{3,2,1,0:T(8,128)(2,1)} %bitcast.3.w_up, bf16[16,1024,2048]{2,1,0:T(8,128)(2,1)} %w_down.1), custom_call_target="tpu_custom_call" | custom-call | tf_op jit(solution)/shard_map/pallas_call | solution.py:386
  96.1 1.0 %copy.8 = bf16[256,2048]{1,0:T(8,128)(2,1)} copy(bf16[256,2048]{1,0:T(8,128)(2,1)S(1)} %shard_map.64) | data formatting | bytes 2097152

commit v7 on v6

--- a/solution.py
+++ b/solution.py
@@ -220,7 +220,7 @@
 
     def begin(k, i):
         rem = (lambda a, b: a % b) if isinstance(i, int) else lax.rem
-        slot = i * PER_BODY if k == 0 else rem(i * PER_BODY + RING1, RING1 + EXTRA) if k == 1 else rem(i * PER_BODY + RING1 - EXTRA, RING1)
+        slot = i * PER_BODY if k == 0 else rem(i * PER_BODY + k * RING1, RING1 + EXTRA) if k < 3 else rem(i * PER_BODY, RING1)
         both = ring1.at[pl.ds(slot, PER_BODY)]
         pltpu.make_async_copy(both, both, w1_sem.at[pair_of(slot)]).wait()
         return [slot + m for m in range(PER_BODY)]
@@ -242,8 +242,9 @@
             for m in range(PER_BODY):
                 e = before * PER_BODY + m
                 down(e, lax.div(e, EPS), lax.rem(e, EPS))
-        if 2 <= k < 4:
-            build_picks((k - 2) * n_body + i)
+        if k == 3:
+            for m in range(2):
+                build_picks(2 * i + m)
 
         def fill(kk, i0):
             for m in range(PER_BODY):
@@ -255,7 +256,10 @@
             when(i < 2)(lambda: fill(1, s0 + EXTRA))
             when(i >= 2)(lambda: fill(2, s0 - EXTRA))
         elif k == 1:
-            when(i >= 2)(lambda: fill(2, s0))
+            fill(2, s0 + EXTRA)
+        elif k == 2:
+            when(i < 2)(lambda: fill(2, s0 + RING1 + EXTRA))
+            when(i >= 4)(lambda: fill(3, s0 - RING1))
         elif final:
             when(s0 + RING1 < here)(lambda: fill(k, s0 + RING1))
         elif static:

time: 97.2 us -> 96.4 us (level)
  no operation moved by 1% of the time
where the time goes in v7:
time: 96.4 us; the launch traced here: 96.3 us
  Pallas kernels  95.3 us (99%)
  local copies, waits for them, and re-layouts  0.97 us (1%)
    pallas_call x1, Pallas kernels, device_step(): pl.pallas_call(layer_kernel, out_shape=pltpu.VMEM((tok_dev, d_model), BF1...  95.3 us

profile of v7, /device:TPU:0, one launch (start us, length us, event | category | flops | bytes accessed | tf_op | source)
XLA Modules:
  0.0 96.3 jit_solution(13380948233155010007)
XLA Ops:
  0.0 95.3 %shard_map.64 = bf16[256,2048]{1,0:T(8,128)(2,1)S(1)} custom-call(bf16[256,2048]{1,0:T(8,128)(2,1)} %tok.1, s32[8,256]{1,0:T(8,128)} %bitcast.4, f32[8,256]{1,0:T(8,128)} %bitcast.5, bf16[16,8,256,1024]{3,2,1,0:T(8,128)(2,1)} %bitcast.2.w_gate, bf16[16,8,256,1024]{3,2,1,0:T(8,128)(2,1)} %bitcast.3.w_up, bf16[16,1024,2048]{2,1,0:T(8,128)(2,1)} %w_down.1), custom_call_target="tpu_custom_call" | custom-call | tf_op jit(solution)/shard_map/pallas_call | solution.py:390
  95.3 1.0 %copy.8 = bf16[256,2048]{1,0:T(8,128)(2,1)} copy(bf16[256,2048]{1,0:T(8,128)(2,1)S(1)} %shard_map.64) | data formatting | bytes 2097152

commit v8 on v7

--- a/solution.py
+++ b/solution.py
@@ -176,11 +176,29 @@
         for p in range(2):
             ring1[RING1 + dev, h, p, pl.ds(r, CAP), :] = jnp.where(t[:, p:p + 1] == at, 1.0, 0.0).astype(BF16)
 
-    def fan(cols, e, n, par):
-        at = lax.broadcasted_iota(jnp.int32, (CAP, n_tok), 0)
+    near, far = (pl.ds(pl.multiple_of(c * 2 * tok_dev, 2 * tok_dev), 2 * tok_dev) for c in (lax.div(me, 2), 1 - lax.div(me, 2)))
+
+    def gather(cols, e, tokens):
+        at = lax.broadcasted_iota(jnp.int32, (CAP, n_tok if tokens is None else 2 * tok_dev), 0)
+        tokens = slice(None) if tokens is None else tokens
+        hot = jnp.concatenate([jnp.where(at == slots[pl.ds(e + m, 1), tokens], 1.0, 0.0).astype(BF16) for m in range(2)], axis=0)
+        return jnp.dot(hot, rows_all[tokens, cols], preferred_element_type=F32)
+
+    def gather_near(col0, width):
+        def pair(i, c):
+            hid[pl.ds(pl.multiple_of(i * 2 * CAP, 2 * CAP), 2 * CAP), pl.ds(col0, width)] = gather(pl.ds(col0, width), i * 2, near).astype(BF16)
+            return c
+
+        lax.fori_loop(0, n_exp // 2, pair, 0)
+
+    def fan(k, e, n, par):
+        cols = block_cols(k)
         for q in range(n // 2):
-            hot = jnp.concatenate([jnp.where(at == slots[pl.ds(e + 2 * q + m, 1), :], 1.0, 0.0).astype(BF16) for m in range(2)], axis=0)
-            x = jnp.dot(hot, rows_all[:, cols], preferred_element_type=F32).astype(BF16)
+            if k < 3:
+                rows = pl.ds((e + 2 * q) * CAP if isinstance(e, int) else pl.multiple_of((e + 2 * q) * CAP, 2 * CAP), 2 * CAP)
+                x = (gather(cols, e + 2 * q, far) + hid[rows, cols].astype(F32)).astype(BF16)
+            else:
+                x = gather(cols, e + 2 * q, None).astype(BF16)
             for u in range(x.shape[1] // KU):
                 xbuf[par, q + u] = x[:, u * KU:(u + 1) * KU]
 
@@ -211,7 +229,8 @@
                     hid[r, cols] = (jax.nn.silu(acts[0]) * acts[1]).astype(BF16)
 
     def take(k):
-        disp_arrival(1, k).wait_recv()
+        if k >= 3:
+            disp_arrival(1, k).wait_recv()
         disp_arrival(2, k).wait_recv()
 
     def hand_on(k):
@@ -235,9 +254,9 @@
         per, n_body = (PER_BODY, n_two) if two else (2 * PER_BODY, n_one)
         par = i % 2 if static else lax.rem(i, 2)
         rings = begin(k, i)
-        ffn_in(i * per, rings, par, two, k == 0, final, FINAL_COLS if final else ffn)
+        ffn_in(i * per, rings, par, two, k == 0, final, 512)
         if nxt is not None:
-            fan(block_cols(nxt[0]), nxt[1] * (PER_BODY if nxt[0] >= 2 else 2 * PER_BODY), PER_BODY if nxt[0] >= 2 else 2 * PER_BODY, 1 - par)
+            fan(nxt[0], nxt[1] * (PER_BODY if nxt[0] >= 2 else 2 * PER_BODY), PER_BODY if nxt[0] >= 2 else 2 * PER_BODY, 1 - par)
         if before is not None:
             for m in range(PER_BODY):
                 e = before * PER_BODY + m
@@ -267,9 +286,13 @@
         else:
             fill(k + lax.div(s0 + RING1, here), lax.rem(s0 + RING1, here))
 
+    for k in range(3):
+        disp_arrival(1, k).wait_recv()
+    gather_near(0, 2 * KU)
     hand_on(0)
+    gather_near(2 * KU, 2 * KU)
     take(0)
-    fan(block_cols(0), 0, 2 * PER_BODY, 0)
+    fan(0, 0, 2 * PER_BODY, 0)
     for k in range(n_kb):
         n_body, final = n_two if k >= 2 else n_one, k == n_kb - 1
         if final:

time: 96.4 us -> 95.7 us (level)
  no operation moved by 1% of the time
where the time goes in v8:
time: 95.7 us; the launch traced here: 95.6 us
  Pallas kernels  94.6 us (99%)
  local copies, waits for them, and re-layouts  0.97 us (1%)
    pallas_call x1, Pallas kernels, device_step(): pl.pallas_call(layer_kernel, out_shape=pltpu.VMEM((tok_dev, d_model), BF1...  94.6 us

profile of v8, /device:TPU:0, one launch (start us, length us, event | category | flops | bytes accessed | tf_op | source)
XLA Modules:
  0.0 95.6 jit_solution(2076572766107380027)
XLA Ops:
  0.0 94.6 %shard_map.64 = bf16[256,2048]{1,0:T(8,128)(2,1)S(1)} custom-call(bf16[256,2048]{1,0:T(8,128)(2,1)} %tok.1, s32[8,256]{1,0:T(8,128)} %bitcast.4, f32[8,256]{1,0:T(8,128)} %bitcast.5, bf16[16,8,256,1024]{3,2,1,0:T(8,128)(2,1)} %bitcast.2.w_gate, bf16[16,8,256,1024]{3,2,1,0:T(8,128)(2,1)} %bitcast.3.w_up, bf16[16,1024,2048]{2,1,0:T(8,128)(2,1)} %w_down.1), custom_call_target="tpu_custom_call" | custom-call | tf_op jit(solution)/shard_map/pallas_call | solution.py:413
  94.6 1.0 %copy.8 = bf16[256,2048]{1,0:T(8,128)(2,1)} copy(bf16[256,2048]{1,0:T(8,128)(2,1)S(1)} %shard_map.64) | data formatting | bytes 2097152
